TPU v7x, 32 devices: a whole 2x2x4 slice. The times are simulated.
32 devices in a mesh: cp: 16 (over z, x, core), tp: 2 (over y).
Axes of the slice: x: 2, y: 2, z: 4, core: 2. Of those that a mesh axis runs over, the one named last changes fastest.
Arguments:
- hidden: bfloat16 [8192, 4096], P('cp', 'tp'), may hold values from -6 to 6
- norm_gain: float32 [4096], replicated, may hold values from 0.5 to 1.5
- w_query: bfloat16 [4096, 4096], P(None, 'tp'), may hold values from -0.140625 to 0.140625
- w_key: bfloat16 [4096, 1024], P(None, 'tp'), may hold values from -4 to 4
- w_value: bfloat16 [4096, 1024], P(None, 'tp'), may hold values from -0.09375 to 0.09375
- w_out: bfloat16 [4096, 4096], P('tp'), may hold values from -0.5 to 0.5
- doc_ids: int32 [8192], P('cp'), may hold values from 0 to 5, never falling along the last dimension, each value on 1 to 6144 neighbouring positions
Outputs:
- updated: bfloat16 [8192, 4096], P('cp', 'tp')
Inputs may be any that keep to these rules, and one draw needn't show every extreme that they name: `doc_ids`: document numbers never fall along the sequence; every document has 1 to 6144 tokens.
All inputs are finite; a program needn't handle non-finite values.
Results may differ from a plain program's by a relative error of at most 0.017.
The roundings to bfloat16 on the way count: a program that leaves them out, or rounds other values in their place, can miss the bound.
Values may be sent and summed in bfloat16 or wider, within the bound.
No kernel may reach another device: no remote copies, remote signals or barrier semaphores. Data moves between devices by JAX's collectives and lax.ppermute only.
A program may use at most 128 MiB of HBM per device.

v0:
```python
import jax
import jax.numpy as jnp
from jax import lax
from jax.sharding import PartitionSpec as P

HEADS = 32
KV_HEADS = 8
HEAD_SIZE = 128


epsilon = 1e-05
rope_base = 500000.0


def rotate(vectors, positions):
    half = HEAD_SIZE // 2
    freqs = rope_base ** (-jnp.arange(half, dtype=jnp.float32) * 2.0 / HEAD_SIZE)
    angles = positions.astype(jnp.float32)[:, None] * freqs[None, :]
    cosine = jnp.cos(angles)[:, None, :]
    sine = jnp.sin(angles)[:, None, :]
    first = vectors[..., :half]
    second = vectors[..., half:]
    return jnp.concatenate(
        [first * cosine - second * sine, second * cosine + first * sine], axis=-1
    )


def attend_block(
    loop_state, query_matrix, query_pos, query_doc, key_matrix, value_matrix, key_pos, key_doc
):
    best, total, running_output = loop_state
    logit_matrix = jnp.einsum(
        "ucpm,ycm->cpuy", query_matrix, key_matrix, preferred_element_type=jnp.float32
    ) * HEAD_SIZE ** (-0.5)
    allowed = (key_pos[None, :] <= query_pos[:, None]) & (key_doc[None, :] == query_doc[:, None])
    masked = jnp.where(allowed, logit_matrix, jnp.float32(-1e30))
    new_best = jnp.maximum(best, jnp.max(masked, axis=-1))
    correction_scale = jnp.exp(best - new_best)
    attention_weights = jnp.where(
        allowed, jnp.exp(logit_matrix - new_best[..., None]), jnp.float32(0.0)
    )
    total = total * correction_scale + jnp.sum(attention_weights, axis=-1)
    running_output = running_output * correction_scale[..., None] + jnp.einsum(
        "sfec,csh->sfeh",
        attention_weights.astype(jnp.bfloat16),
        value_matrix,
        preferred_element_type=jnp.float32,
    )
    return (new_best, total, running_output)


def shards(hidden, norm_gain, w_query, w_key, w_value, w_out, doc_ids):
    tok_rows = hidden.shape[0]
    half_rows = tok_rows // 2
    width = norm_gain.shape[0]
    group = HEADS // KV_HEADS
    local_kv = w_key.shape[1] // HEAD_SIZE
    query_cols = w_query.shape[1]
    key_cols = w_key.shape[1]
    wide_local = hidden.astype(jnp.float32)
    squares = lax.psum(jnp.sum(wide_local * wide_local, axis=1), "tp")
    inverse_rms = lax.rsqrt(squares / width + epsilon)[:, None]
    piece = lax.all_gather(hidden, "tp", axis=1, tiled=True)
    normed_piece = (piece.astype(jnp.float32) * inverse_rms * norm_gain[None, :]).astype(
        jnp.bfloat16
    )
    projected = jnp.concatenate(
        [
            jnp.dot(normed_piece, w_query, preferred_element_type=jnp.float32),
            jnp.dot(normed_piece, w_key, preferred_element_type=jnp.float32),
            jnp.dot(normed_piece, w_value, preferred_element_type=jnp.float32),
        ],
        axis=1,
    )
    cp_rank = lax.axis_index("cp")
    positions = cp_rank * tok_rows + jnp.arange(tok_rows, dtype=jnp.int32)
    query_raw = projected[:, :query_cols].reshape(tok_rows, local_kv * group, HEAD_SIZE)
    key_raw = projected[:, query_cols : query_cols + key_cols].reshape(
        tok_rows, local_kv, HEAD_SIZE
    )
    query_matrix = (
        rotate(query_raw, positions)
        .astype(jnp.bfloat16)
        .reshape(tok_rows, local_kv, group, HEAD_SIZE)
    )
    keys_flat = rotate(key_raw, positions).astype(jnp.bfloat16).reshape(tok_rows, key_cols)
    values_flat = projected[:, query_cols + key_cols :].astype(jnp.bfloat16)
    query_doc = doc_ids.astype(jnp.float32)
    docs_flat = query_doc.astype(jnp.bfloat16)
    first_queries = query_matrix[:half_rows]
    first_pos = positions[:half_rows]
    first_doc = query_doc[:half_rows]
    second_queries = query_matrix[half_rows:]
    second_doc = query_doc[half_rows:]
    second_start = cp_rank * tok_rows + half_rows
    second_pos = second_start + jnp.arange(half_rows, dtype=jnp.int32)
    last_first = cp_rank * tok_rows + half_rows - 1
    last_second = second_start + half_rows - 1
    init_half = (
        jnp.full((local_kv, group, half_rows), -1e30, jnp.float32),
        jnp.zeros((local_kv, group, half_rows), jnp.float32),
        jnp.zeros((local_kv, group, half_rows, HEAD_SIZE), jnp.float32),
    )
    init = (init_half, init_half)
    key_piece = lax.all_gather(keys_flat, "cp", axis=0, tiled=True)
    value_piece = lax.all_gather(values_flat, "cp", axis=0, tiled=True)
    doc_piece = lax.all_gather(docs_flat, "cp", axis=0, tiled=True)
    count = key_piece.shape[0]

    def inner(index, state):
        first_state, second_state = state
        offset = index * tok_rows
        key_blk = lax.dynamic_slice_in_dim(key_piece, offset, tok_rows, 0).reshape(
            tok_rows, local_kv, HEAD_SIZE
        )
        value_blk = lax.dynamic_slice_in_dim(value_piece, offset, tok_rows, 0).reshape(
            tok_rows, local_kv, HEAD_SIZE
        )
        key_doc = lax.dynamic_slice_in_dim(doc_piece, offset, tok_rows, 0).astype(jnp.float32)
        key_pos = offset + jnp.arange(tok_rows, dtype=jnp.int32)

        def attend_first(inner_state):
            return attend_block(
                inner_state,
                first_queries,
                first_pos,
                first_doc,
                key_blk,
                value_blk,
                key_pos,
                key_doc,
            )

        def attend_second(inner_state):
            return attend_block(
                inner_state,
                second_queries,
                second_pos,
                second_doc,
                key_blk,
                value_blk,
                key_pos,
                key_doc,
            )

        first_state = lax.cond(
            offset <= last_first, attend_first, lambda inner_state: inner_state, first_state
        )
        second_state = lax.cond(
            offset <= last_second, attend_second, lambda inner_state: inner_state, second_state
        )
        return (first_state, second_state)

    final = lax.fori_loop(0, count // tok_rows, inner, init)

    def finish(state):
        result = state[2] / state[1][..., None]
        return (
            jnp.transpose(result, (2, 0, 1, 3)).reshape(half_rows, query_cols).astype(jnp.bfloat16)
        )

    attended_first = finish(final[0])
    attended_second = finish(final[1])
    attended = jnp.concatenate([attended_first, attended_second], axis=0)
    terms = jnp.dot(attended, w_out, preferred_element_type=jnp.float32)
    summed = lax.psum_scatter(terms.astype(jnp.bfloat16), "tp", scatter_dimension=1, tiled=True)
    return summed


def solution(mesh):
    in_specs = (
        P("cp", "tp"),
        P(),
        P(None, "tp"),
        P(None, "tp"),
        P(None, "tp"),
        P("tp", None),
        P("cp"),
    )
    out_specs = P("cp", "tp")
    return jax.shard_map(shards, mesh=mesh, in_specs=in_specs, out_specs=out_specs, check_vma=False)
```

profile of v0, /device:TPU:0, one launch (start us, length us, event | category | flops | bytes accessed | tf_op | source)
XLA Modules:
  0.0 622.3 jit_solution(9094426565222155319)
XLA Ops:
  7.3 2.1 multiply_reduce_fusion
  9.4 5.9 psum.7
  15.8 52.5 %all-gather.5.cloned.1.call-done = bf16[512,4096]{1,0:T(8,128)(2,1)} async-done(((bf16[512,2048]{1,0:T(8,128)(2,1)}), bf16[512,4096]{1,0:T(8,128)(2,1)}) %all-gather.5.cloned.1.call-update) | async-done | bytes 4194320 | tf_op jit(solution)/shard_map/all_gather | solution.py:63
  68.4 5.9 fusion.44
  75.4 6.6 %convolution_convert_fusion.1 = bf16[512,512]{1,0:T(8,128)(2,1)} fusion(bf16[4096,512]{1,0:T(8,128)(2,1)} %param.17, bf16[512,4096]{1,0:T(8,128)(2,1)} %all-gather.5.cloned.1.call-done, f32[4096]{0:T(1024)S(1)} %copy-done.7, f32[512]{0:T(512)S(1)} %add_rsqrt_fusion), kind=kOutput, calls=%fused_computation.61 | convolution fusion | flops 2156134400 | bytes 8931328 | tf_op jit(solution)/shard_map/dot_general | solution.py:71
  82.4 22.4 %all-gather = bf16[16,1,512]{2,1,0:T(2,128)(2,1)S(1)} all-gather(bf16[1,1,512]{2,1,0:T(2,128)(2,1)S(1)} %reshape.106), channel_id=1, replica_groups=mesh['cp'=16,'tp'=2] {'cp'}, dimensions={0}, use_global_device_ids=true | all-gather | bytes 17408 | tf_op jit(solution)/shard_map/all_gather | solution.py:107
  105.0 13.1 %convolution_bitcast_fusion = f32[64,8,16,128]{3,1,2,0:T(8,128)S(1)} fusion(bf16[4096,2048]{1,0:T(8,128)(2,1)} %param.15, bf16[512,4096]{1,0:T(8,128)(2,1)} %all-gather.5.cloned.1.call-done, f32[4096]{0:T(1024)S(1)} %copy-done.7, f32[512]{0:T(512)S(1)} %add_rsqrt_fusion), kind=kOutput, calls=%fused_computation.53 | convolution fusion | flops 8598323200 | bytes 25184256 | tf_op jit(solution)/shard_map/dot_general | solution.py:69
  119.0 1.6 add_convert_fusion
  122.3 31.2 %all-gather.7.cloned.1.call-done = bf16[8192,512]{0,1:T(8,128)(2,1)} async-done(((bf16[512,512]{0,1:T(8,128)(2,1)}), bf16[8192,512]{0,1:T(8,128)(2,1)}) %all-gather.7.cloned.1.call-update) | async-done | bytes 8388624 | tf_op jit(solution)/shard_map/all_gather | solution.py:105
  153.5 74.7 %all-gather.9.cloned.1.call-done = bf16[8192,512]{1,0:T(8,128)(2,1)} async-done(((bf16[512,512]{1,0:T(8,128)(2,1)}), bf16[8192,512]{1,0:T(8,128)(2,1)}) %all-gather.9.cloned.1.call-update) | async-done | bytes 8388624 | tf_op jit(solution)/shard_map/all_gather | solution.py:106
  229.7 1.6 broadcast_in_dim.42.clone
  231.3 68.3 %while.24 = (s32[]{:T(128)}, f32[4,4,256]{2,1,0:T(4,128)S(1)}, f32[4,4,256]{2,1,0:T(4,128)S(1)}, f32[4,4,256,128]{3,2,1,0:T(8,128)}, f32[4,4,256]{2,1,0:T(4,128)...) while((s32[]{:T(128)}, f32[4,4,256]{2,1,0:T(4,128)S(1)}, ...), condition=%wide.region_11.12_spmd.clone, body=%wide.region_2.11_spmd.clone.sunk | while | flops 2196522240 | bytes 105403112 | solution.py:154
  234.5 8.1 %conditional.6 = ((f32[4,4,256]{2,1,0:T(4,128)S(1)}, f32[4,4,256]{2,1,0:T(4,128)S(1)}, f32[4,4,256,128]{3,2,1,0:T(8,128)})) conditional(s32[]{:T(128)} %convert_element_type.128, (f32[4,4,256]{2,1,0:T(4,128)S(1)}, f32[4,4,256]{2,1,0:T(4,128)S(1)}, f32[4,4,256,128]{3,2,1,0:T(8,128)}) %tuple.72, (s32[512]{0:T(512)S(1)}, s32[256]{0:T(256)S(1)}, ...), branch_computations={%region_3.0_spmd, %region_4.6_spmd} | conditional | flops 1098260480 | bytes 51124340 | solution.py:146
  236.3 1.7 fusion.6
  238.1 3.2 multiply_add_fusion
  242.6 8.1 %conditional.7 = ((f32[4,4,256]{2,1,0:T(4,128)S(1)}, f32[4,4,256]{2,1,0:T(4,128)S(1)}, f32[4,4,256,128]{3,2,1,0:T(8,128)})) conditional(s32[]{:T(128)} %convert_element_type.129, (f32[4,4,256]{2,1,0:T(4,128)S(1)}, f32[4,4,256]{2,1,0:T(4,128)S(1)}, f32[4,4,256,128]{3,2,1,0:T(8,128)}) %tuple.74, (s32[512]{0:T(512)S(1)}, s32[]{:T(128)}, ...), branch_computations={%region_7.7_spmd, %region_8.10_spmd} | conditional | flops 1098260736 | bytes 51126392 | solution.py:149
  242.8 1.6 fusion.20
  244.4 1.7 fusion.24
  246.1 3.2 multiply_add_fusion.2
  299.6 1.9 copy.40
  301.5 2.9 copy.39
  304.4 2.1 divide_convert_fusion
  306.5 14.0 %convolution_convert_fusion = bf16[512,4096]{1,0:T(8,128)(2,1)} fusion(bf16[2048,4096]{1,0:T(8,128)(2,1)} %param.18, bf16[256,2048]{0,1:T(8,128)(2,1)S(1)} %bitcast.110, bf16[256,2048]{0,1:T(8,128)(2,1)S(1)} %bitcast.111), kind=kOutput, calls=%fused_computation.49 | convolution fusion | flops 8596226048 | bytes 23068672 | tf_op jit(solution)/shard_map/dot_general | solution.py:165
  320.5 295.2 %reduce-scatter.2.cloned.1.call-done = bf16[512,2048]{1,0:T(8,128)(2,1)} async-done(((bf16[512,4096]{1,0:T(8,128)(2,1)}), bf16[512,2048]{1,0:T(8,128)(2,1)}) %reduce-scatter.2.cloned.1.call-update) | async-done | bytes 2097168 | tf_op jit(solution)/shard_map/reduce_scatter | solution.py:166
  (184 shorter events, 63.7 us)
Async XLA Ops:
  6.5 61.8 %copy-start.7 = (f32[4096]{0:T(1024)S(1)}, f32[4096]{0:T(1024)}, u32[]{:S(2)}) copy-start(f32[4096]{0:T(1024)} %param.14) | copy-start | bytes 49156
  6.5 61.8 %all-gather.5.cloned.1.call-start = ((), (), s32[]{:S(2)}) async-start(), calls=%async_computation.1 | async-start | bytes 6291456 | tf_op jit(solution)/shard_map/all_gather | solution.py:63
  7.3 146.2 %all-gather.7.cloned.1.call-start = ((), (), s32[]{:S(2)}) async-start(), calls=%async_computation.2 | async-start | bytes 8912896 | tf_op jit(solution)/shard_map/all_gather | solution.py:105
  75.3 7.0 %copy-start.6 = (s32[512]{0:T(512)S(1)}, s32[512]{0:T(512)}, u32[]{:S(2)}) copy-start(s32[512]{0:T(512)} %param.19) | copy-start | bytes 6148
  75.4 152.8 %all-gather.9.cloned.1.call-start = ((), (), s32[]{:S(2)}) async-start(), calls=%async_computation.3 | async-start | bytes 8912896 | tf_op jit(solution)/shard_map/all_gather | solution.py:106
  82.1 533.7 %reduce-scatter.2.cloned.1.call-start = ((), (), s32[]{:S(2)}) async-start(), calls=%async_computation.4 | async-start | bytes 6291456 | tf_op jit(solution)/shard_map/reduce_scatter | solution.py:166
  236.3 1.8 copy-start
  236.3 1.8 copy-start.2
  241.2 1.3 copy-start.3
  244.4 1.8 copy-start.1
  244.4 1.8 copy-start.4
  249.3 1.3 copy-start.5
Sparse Core Ops, SparseCore 0:
  8.9 59.4 all-gather.4
  75.5 77.9 all-gather.6
  155.6 72.4 all-gather.8
  320.7 295.0 reduce-scatter.1
where the time goes:
time: 625 us; the launch traced here: 622 us
  waiting for transfers between devices  454 us (73%)
  local copies, waits for them, and re-layouts  63.1 us (10%)
  matrix products  49.1 us (8%)
  blocking collectives  28.3 us (5%)
  other arithmetic  13.6 us (2%)
  between operations  13.3 us (2%)
    reduce_scatter x1, waiting for transfers between devices, shards(): lax.psum_scatter(terms.astype(jnp.bfloat16), 'tp', scatter_dimension=1, t...  295 us
    all_gather x1, waiting for transfers between devices, shards(): value_piece = lax.all_gather(values_flat, 'cp', axis=0, tiled=True)  74.7 us
    all_gather x1, waiting for transfers between devices, shards(): piece = lax.all_gather(hidden, 'tp', axis=1, tiled=True)  52.5 us
    dynamic_slice x32, local copies, waits for them, and re-layouts, inner(): lax.dynamic_slice_in_dim(value_piece, offset, tok_rows, 0)  33.5 us
    all_gather x1, waiting for transfers between devices, shards(): key_piece = lax.all_gather(keys_flat, 'cp', axis=0, tiled=True)  31.2 us
    all_gather x1, blocking collectives, shards(): doc_piece = lax.all_gather(docs_flat, 'cp', axis=0, tiled=True)  22.4 us
    dynamic_slice x16, local copies, waits for them, and re-layouts, inner(): lax.dynamic_slice_in_dim(key_piece, offset, tok_rows, 0)  17.2 us
    dot_general x1, matrix products, shards(): terms = jnp.dot(attended, w_out, preferred_element_type=jnp.float32)  14 us
  transfers between devices with their start and end apart: 4, of which 4 were waited for; matrix products, arithmetic and copies ran while one was open for 4% of the time, Pallas kernels for 0%

commit v1 on v0

v1 whole, which is shorter than its diff:
```python
import functools

import jax
import jax.numpy as jnp
from jax import lax
from jax.experimental import pallas as pl
from jax.experimental.pallas import tpu as pltpu
from jax.sharding import PartitionSpec as P


HEAD_SIZE = 128

epsilon = 1e-05
rope_base = 500000.0
MASKED = -1e30
LOG2E = 1.4426950408889634
PLANE = 4
VMEM = 32 * 1024 * 1024
GRANT = 24 * 1024 * 1024


def turn(vectors, cosine, sine):
    heads = [
        vectors[:, low : low + HEAD_SIZE] for low in range(0, vectors.shape[1], HEAD_SIZE)
    ]
    return [
        (head * cosine + pltpu.roll(head, HEAD_SIZE // 2, 1) * sine).astype(jnp.bfloat16)
        for head in heads
    ]


def key_value_kernel(n_tp, block, info, *refs):
    pieces, refs = refs[:n_tp], refs[n_tp:]
    gain_ref, cos_ref, sin_ref, key_hbm, value_hbm, out_ref, normed_hbm = refs[:7]
    held, normed_ref, key_ref, value_ref, piece_sem, weight_sem, out_sem = refs[7:]
    tokens, features = pieces[0].shape
    width = features * n_tp
    steps = key_hbm.shape[1] // block
    piece_copies = [
        pltpu.make_async_copy(piece, held.at[i], piece_sem.at[i]) for i, piece in enumerate(pieces)
    ]
    for copy in piece_copies:
        copy.start()
    weight_copies = []
    for step in range(steps):
        columns = pl.ds(step * block, block)
        for at, (source, target) in enumerate(((key_hbm, key_ref), (value_hbm, value_ref))):
            copy = pltpu.make_async_copy(
                source.at[:, columns], target.at[step], weight_sem.at[2 * step + at]
            )
            copy.start()
            weight_copies.append(copy)
    total = None
    for i, copy in enumerate(piece_copies):
        copy.wait()
        wide = held[i].astype(jnp.float32)
        squares = jnp.sum(wide * wide, axis=1, keepdims=True)
        total = squares if total is None else total + squares
    scale = lax.rsqrt(total / width + epsilon)
    for i in range(n_tp):
        owner = lax.rem(info[10] - i + n_tp, n_tp)
        columns = pl.ds(pl.multiple_of(owner * features, HEAD_SIZE), features)
        normed_ref[:, columns] = (
            held[i].astype(jnp.float32) * scale * gain_ref[0:1, columns]
        ).astype(jnp.bfloat16)
    normed_copy = pltpu.make_async_copy(normed_ref, normed_hbm, out_sem)
    normed_copy.start()
    heads = block // HEAD_SIZE
    for step in range(steps):
        weight_copies[2 * step].wait()
        keys = jnp.dot(normed_ref[...], key_ref[step], preferred_element_type=jnp.float32)
        turned = turn(keys, cos_ref[...], sin_ref[...])
        weight_copies[2 * step + 1].wait()
        values = jnp.dot(normed_ref[...], value_ref[step], preferred_element_type=jnp.float32)
        for head in range(heads):
            out_ref[step * heads + head, :, :HEAD_SIZE] = turned[head]
            mine = values[:, head * HEAD_SIZE : (head + 1) * HEAD_SIZE]
            for low in range(0, tokens, HEAD_SIZE):
                out_ref[step * heads + head, low : low + HEAD_SIZE, HEAD_SIZE:] = mine[
                    low : low + HEAD_SIZE, :
                ].T.astype(jnp.bfloat16)
    normed_copy.wait()


def project_keys(info, pieces, gain, cosine, sine, w_key, w_value):
    n_tp = len(pieces)
    tokens, features = pieces[0].shape
    depth, columns = w_key.shape
    block = min(2 * HEAD_SIZE, columns)
    steps = columns // block
    away = pl.BlockSpec(memory_space=pl.ANY)
    near = pl.BlockSpec(memory_space=pltpu.VMEM)
    return pl.pallas_call(
        functools.partial(key_value_kernel, n_tp, block),
        in_specs=[pl.BlockSpec(memory_space=pltpu.SMEM)]
        + [away] * n_tp
        + [near, near, near, away, away],
        out_specs=[near, away],
        out_shape=[
            jax.ShapeDtypeStruct((columns // HEAD_SIZE, tokens, 2 * HEAD_SIZE), jnp.bfloat16),
            jax.ShapeDtypeStruct((tokens, depth), jnp.bfloat16),
        ],
        scratch_shapes=[
            pltpu.VMEM((n_tp, tokens, features), jnp.bfloat16),
            pltpu.VMEM((tokens, depth), jnp.bfloat16),
            pltpu.VMEM((steps, depth, block), jnp.bfloat16),
            pltpu.VMEM((steps, depth, block), jnp.bfloat16),
            pltpu.SemaphoreType.DMA((n_tp,)),
            pltpu.SemaphoreType.DMA((2 * steps,)),
            pltpu.SemaphoreType.DMA,
        ],
        compiler_params=pltpu.CompilerParams(vmem_limit_bytes=VMEM),
        cost_estimate=pl.CostEstimate(
            flops=4 * tokens * depth * columns, bytes_accessed=4 * depth * columns, transcendentals=0
        ),
        name="project_keys",
    )(info, *pieces, gain, cosine, sine, w_key, w_value)


def product_kernel(block, rotary, offset, *refs):
    if rotary:
        cos_ref, sin_ref, refs = refs[0], refs[1], refs[2:]
    x_hbm, weight_hbm, out_ref, x_ref, held, x_sem, weight_sem = refs
    steps = out_ref.shape[1] // block

    def copy(step):
        columns = pl.ds(pl.multiple_of(offset[0] + step * block, HEAD_SIZE), block)
        return pltpu.make_async_copy(
            weight_hbm.at[:, columns], held.at[step], weight_sem.at[step]
        )

    x_copy = pltpu.make_async_copy(x_hbm, x_ref, x_sem)
    x_copy.start()
    for step in range(steps):
        copy(step).start()
    x_copy.wait()

    def body(step, _):
        copy(step).wait()
        result = jnp.dot(x_ref[...], held[step], preferred_element_type=jnp.float32)
        columns = pl.ds(pl.multiple_of(step * block, block), block)
        if rotary:
            result = jnp.concatenate(turn(result, cos_ref[...], sin_ref[...]), axis=1)
        out_ref[:, columns] = result.astype(jnp.bfloat16)
        return 0

    lax.fori_loop(0, steps, body, 0)


def product(x, weights, offset, columns, turns=None):
    tokens, depth = x.shape
    block = min(4 * HEAD_SIZE, columns)
    steps = columns // block
    away = pl.BlockSpec(memory_space=pl.ANY)
    near = pl.BlockSpec(memory_space=pltpu.VMEM)
    turns = turns or ()
    return pl.pallas_call(
        functools.partial(product_kernel, block, bool(turns)),
        in_specs=[pl.BlockSpec(memory_space=pltpu.SMEM)] + [near] * len(turns) + [away, away],
        out_specs=near,
        out_shape=jax.ShapeDtypeStruct((tokens, columns), jnp.bfloat16),
        scratch_shapes=[
            pltpu.VMEM((tokens, depth), jnp.bfloat16),
            pltpu.VMEM((steps, depth, block), jnp.bfloat16),
            pltpu.SemaphoreType.DMA,
            pltpu.SemaphoreType.DMA((steps,)),
        ],
        compiler_params=pltpu.CompilerParams(vmem_limit_bytes=VMEM),
        cost_estimate=pl.CostEstimate(
            flops=2 * tokens * depth * columns,
            bytes_accessed=2 * depth * columns,
            transcendentals=0,
        ),
        name="project_queries" if turns else "partial_product",
    )(offset, *turns, x, weights)


def attend_kernel(group, backs, part, first, last, info, start_ref, q_ref, *refs):
    sets, refs = refs[: 2 * len(backs)], refs[2 * len(backs) :]
    if not first:
        acc_in, stat_in, refs = refs[0], refs[1], refs[2:]
    if last:
        out_ref, refs = refs[0], refs[1:]
    acc, stat, rows, key_rows, value_cols, bias, score_a, score_b, units = refs
    scale = HEAD_SIZE**-0.5 * LOG2E
    queries = q_ref.shape[0]
    size = sets[0].shape[0] * sets[0].shape[2] // 2
    tiles = group // 2
    base, low_start, high_start = info[0], info[1 + 2 * part], info[2 + 2 * part]
    layer, inner = info[8], info[9]
    query_low = base + part * queries
    query_high = query_low + queries - 1

    if first:
        acc[...] = jnp.zeros(acc.shape, jnp.float32)
        stat[0, :tiles, :] = jnp.full((tiles, 2 * queries), MASKED, jnp.float32)
        stat[0, tiles:, :] = jnp.zeros((tiles, 2 * queries), jnp.float32)
    else:
        acc[...] = acc_in[...]
        stat[...] = stat_in[...]
    for tile in range(tiles):
        for side in range(2):
            head = 2 * tile + side
            rows[tile, side * queries : (side + 1) * queries, :] = q_ref[
                :, head * HEAD_SIZE : (head + 1) * HEAD_SIZE
            ]

    plain_count, masked_count = jnp.int32(0), jnp.int32(0)
    for at, back in enumerate(backs):
        for array in range(2):
            for half in range(2):
                unit = 4 * at + 2 * array + half
                block = (layer - back) * PLANE + (inner ^ (array + 2 * half))
                key_low = block * size
                key_high = key_low + size - 1
                need = (layer >= back) & (key_low <= query_high) & (key_high >= low_start)
                plain = need & (key_high <= query_low) & (key_low >= high_start)
                units[0, plain_count] = unit
                plain_count = plain_count + plain.astype(jnp.int32)
                units[1, masked_count] = unit
                units[2, masked_count] = key_low
                masked_count = masked_count + (need & ~plain).astype(jnp.int32)

                @pl.when(need)
                def _():
                    source = sets[2 * at + array]
                    piece = source.shape[2]
                    for i in range(size // piece):
                        entry = half * (size // piece) + i
                        key_rows[unit, i * piece : (i + 1) * piece, :] = source[
                            entry, 0, :, :HEAD_SIZE
                        ]
                        for low in range(0, piece, HEAD_SIZE):
                            at_token = i * piece + low
                            value_cols[unit, :, at_token : at_token + HEAD_SIZE] = source[
                                entry, 0, low : low + HEAD_SIZE, HEAD_SIZE:
                            ]

    @pl.when(pl.program_id(0) == 0)
    def _():
        def fill(index, _):
            shape = (size, queries)
            key_at = units[2, index] + lax.broadcasted_iota(jnp.int32, shape, 0)
            query_at = query_low + lax.broadcasted_iota(jnp.int32, shape, 1)
            allowed = (key_at >= start_ref[0:1, :]) & (key_at <= query_at)
            bias[index] = jnp.where(allowed, 0.0, MASKED)
            return 0

        lax.fori_loop(0, masked_count, fill, 0)

    def sweep(which, count, masked):
        def scores(index, tile, buffer):
            s = lax.dot_general(
                key_rows[units[which, index]],
                rows[tile],
                (((1,), (1,)), ((), ())),
                preferred_element_type=jnp.float32,
            )
            if masked:
                once = bias[index]
                s = s + jnp.concatenate([once, once], axis=1)
            buffer[...] = s
            return jnp.max(s, axis=0, keepdims=True)

        def weigh(index, tile, buffer, peak):
            old = stat[0, tile : tile + 1, :]
            new = jnp.maximum(old, peak)
            shrink = jnp.exp2((old - new) * scale)
            weights = jnp.exp2((buffer[...] - new) * scale)
            added = jnp.dot(
                value_cols[units[which, index]],
                weights.astype(jnp.bfloat16),
                preferred_element_type=jnp.float32,
            )
            acc[0, tile] = acc[0, tile] * shrink + added
            total = stat[0, tiles + tile : tiles + tile + 1, :]
            stat[0, tiles + tile : tiles + tile + 1, :] = total * shrink + jnp.sum(
                weights, axis=0, keepdims=True
            )
            stat[0, tile : tile + 1, :] = new

        def step(index, peak):
            following = jnp.minimum(index + 1, count - 1)
            for tile in range(0, tiles, 2):
                peak_b = scores(index, tile + 1, score_b)
                weigh(index, tile, score_a, peak)
                if tile + 2 < tiles:
                    peak = scores(index, tile + 2, score_a)
                else:
                    peak = scores(following, 0, score_a)
                weigh(index, tile + 1, score_b, peak_b)
            return peak

        @pl.when(count > 0)
        def _():
            lax.fori_loop(0, count, step, scores(0, 0, score_a))

    sweep(0, plain_count, False)
    sweep(1, masked_count, True)

    if last:
        for tile in range(tiles):
            done = acc[0, tile] / stat[0, tiles + tile : tiles + tile + 1, :]
            for side in range(2):
                head = 2 * tile + side
                out_ref[:, head * HEAD_SIZE : (head + 1) * HEAD_SIZE] = done[
                    :, side * queries : (side + 1) * queries
                ].T.astype(jnp.bfloat16)


def attend(info, start, queries, sets, backs, part, state, local_kv, last):
    tokens, columns = queries.shape
    group = columns // HEAD_SIZE // local_kv
    tiles = group // 2
    first = state is None
    arrays = [array for entry in sets for array in entry]
    entries, _, piece, _ = arrays[0].shape
    size = entries * piece // 2
    count = 2 * len(arrays)
    acc_shape = (1, tiles, HEAD_SIZE, 2 * tokens)
    stat_shape = (1, 2 * tiles, 2 * tokens)
    acc_block = pl.BlockSpec(acc_shape, lambda g, s: (g, 0, 0, 0))
    stat_block = pl.BlockSpec(stat_shape, lambda g, s: (g, 0, 0))
    q_block = pl.BlockSpec((tokens, group * HEAD_SIZE), lambda g, s: (0, g))
    in_specs = [pl.BlockSpec((8, tokens), lambda g, s: (0, part)), q_block]
    in_specs += [
        pl.BlockSpec((entries, 1, piece, 2 * HEAD_SIZE), lambda g, s: (0, g, 0, 0)) for _ in arrays
    ]
    operands = [info, start, queries, *arrays]
    scratch = [
        pltpu.VMEM((tiles, 2 * tokens, HEAD_SIZE), jnp.bfloat16),
        pltpu.VMEM((count, size, HEAD_SIZE), jnp.bfloat16),
        pltpu.VMEM((count, HEAD_SIZE, size), jnp.bfloat16),
        pltpu.VMEM((count, size, tokens), jnp.float32),
        pltpu.VMEM((size, 2 * tokens), jnp.float32),
        pltpu.VMEM((size, 2 * tokens), jnp.float32),
        pltpu.SMEM((3, count + 1), jnp.int32),
    ]
    aliases = {}
    if not first:
        in_specs += [acc_block, stat_block]
        operands += list(state)
        if not last:
            aliases = {len(operands) - 2: 0, len(operands) - 1: 1}
    if last:
        out_specs = [q_block]
        out_shape = [jax.ShapeDtypeStruct(queries.shape, jnp.bfloat16)]
        scratch = [
            pltpu.VMEM(acc_shape, jnp.float32),
            pltpu.VMEM(stat_shape, jnp.float32),
        ] + scratch
    else:
        out_specs = [acc_block, stat_block]
        out_shape = [
            jax.ShapeDtypeStruct((local_kv, *acc_shape[1:]), jnp.float32),
            jax.ShapeDtypeStruct((local_kv, *stat_shape[1:]), jnp.float32),
        ]
    return pl.pallas_call(
        functools.partial(attend_kernel, group, backs, part, first, last),
        grid_spec=pltpu.PrefetchScalarGridSpec(
            num_scalar_prefetch=1,
            grid=(local_kv,),
            in_specs=in_specs,
            out_specs=out_specs,
            scratch_shapes=scratch,
        ),
        out_shape=out_shape,
        input_output_aliases=aliases,
        compiler_params=pltpu.CompilerParams(
            dimension_semantics=("arbitrary",), vmem_limit_bytes=GRANT
        ),
        cost_estimate=pl.CostEstimate(
            flops=8 * columns * tokens * size * count,
            bytes_accessed=8 * 1024 * 1024,
            transcendentals=0,
        ),
        name="attend",
    )(*operands)


def set_groups(layers):
    return [(0,)] + ([(1, 2)] if layers > 2 else []) + [(back,) for back in range(3, layers)]


def sublayer(n_cp, n_tp, parts, hidden, norm_gain, w_query, w_key, w_value, w_out, doc_ids):
    tokens, features = hidden.shape
    local_kv = w_key.shape[1] // HEAD_SIZE
    layers = n_cp // PLANE
    piece = tokens // parts
    cp_rank = lax.axis_index("cp")
    tp_rank = lax.axis_index("tp")

    def tp_shift(array, shift):
        return lax.ppermute(array, "tp", [(i, (i + shift) % n_tp) for i in range(n_tp)])

    def cp_shift(array, shift):
        return lax.ppermute(array, "cp", [(i, i + shift) for i in range(n_cp - shift)])

    gathered = []
    for part in range(parts):
        mine = hidden[part * piece : (part + 1) * piece]
        gathered.append([mine] + [tp_shift(mine, shift) for shift in range(1, n_tp)])

    buckets = jnp.arange(128, dtype=jnp.int32)
    counts = jnp.sum((doc_ids[:, None] == buckets[None, :]).astype(jnp.int32), axis=0)
    running = counts
    reach = 1
    while reach < n_cp:
        running = running + cp_shift(running, reach)
        reach *= 2
    before = running - counts
    base = cp_rank * tokens
    earlier = jnp.sum((doc_ids[None, :] < doc_ids[:, None]).astype(jnp.int32), axis=1)
    carried = jnp.sum(jnp.where(buckets == doc_ids[0], before, 0))
    start = base + earlier - jnp.where(doc_ids == doc_ids[0], carried, 0)
    start_rows = jnp.broadcast_to(start[None, :], (8, tokens))
    ends = []
    for part in range(parts):
        ends += [start[part * piece], start[(part + 1) * piece - 1]]
    entries = [base, *ends] + [0] * (7 - len(ends))
    entries += [lax.div(cp_rank, PLANE), lax.rem(cp_rank, PLANE), tp_rank]
    slots = jnp.arange(16, dtype=jnp.int32)
    info = jnp.zeros((16,), jnp.int32)
    for slot, entry in enumerate(entries):
        info = jnp.where(slots == slot, entry, info)

    lanes = jnp.arange(HEAD_SIZE, dtype=jnp.int32)
    half = HEAD_SIZE // 2
    freqs = rope_base ** (-jnp.where(lanes < half, lanes, lanes - half) * 2.0 / HEAD_SIZE)
    positions = base + jnp.arange(tokens, dtype=jnp.int32)
    angles = positions.astype(jnp.float32)[:, None] * freqs[None, :]
    cosine = jnp.cos(angles)
    sine = jnp.where(lanes < half, -1.0, 1.0)[None, :] * jnp.sin(angles)
    gain = norm_gain[None, :]

    near = [[] for _ in range(layers)]
    far = [[] for _ in range(layers)]
    q_parts = []
    cross = [(i, i ^ 2) for i in range(n_cp)]
    own_cross = [(i, i ^ 2) for i in range(n_cp) if not i & 2]
    for part in range(parts):
        cut = slice(part * piece, (part + 1) * piece)
        block, normed = project_keys(
            info, gathered[part], gain, cosine[cut], sine[cut], w_key, w_value
        )
        for back in range(layers):
            if back == 0:
                here = block
            elif back <= 2:
                here = cp_shift(block, back * PLANE)
            else:
                here = cp_shift(near[back - 1][part], PLANE)
            near[back].append(here)
            far[back].append(lax.ppermute(here, "cp", cross if back else own_cross))
        q_parts.append(
            product(normed, w_query, info[15:], w_query.shape[1], (cosine[cut], sine[cut]))
        )
    sets = []
    swap = [(i, i ^ 1) for i in range(n_cp)]
    for back in range(layers):
        local = jnp.stack(near[back] + far[back])
        sets.append([local, lax.ppermute(local, "cp", swap)])

    states = [None] * parts
    for backs in set_groups(layers):
        for part in range(parts):
            states[part] = attend(
                info, start_rows, q_parts[part], [sets[back] for back in backs], backs, part,
                states[part], local_kv, backs[-1] == layers - 1,
            )

    outs = []
    for part in range(parts):
        attended = states[part][0]
        received = []
        for shift in range(1, n_tp):
            owner = lax.rem(info[10:11] + shift, n_tp)
            received.append(
                tp_shift(product(attended, w_out, owner * features, features), shift)
            )
        own = product(attended, w_out, info[10:11] * features, features)
        mixed = own.astype(jnp.float32)
        for other in received:
            mixed = mixed + other.astype(jnp.float32)
        outs.append(mixed.astype(jnp.bfloat16))
    return jnp.concatenate(outs, axis=0)


def solution(mesh):
    in_specs = (
        P("cp", "tp"),
        P(),
        P(None, "tp"),
        P(None, "tp"),
        P(None, "tp"),
        P("tp", None),
        P("cp"),
    )
    out_specs = P("cp", "tp")
    body = functools.partial(sublayer, mesh.shape["cp"], mesh.shape["tp"], 2)
    return jax.shard_map(body, mesh=mesh, in_specs=in_specs, out_specs=out_specs, check_vma=False)
```

time: 625 us -> 330 us (0.53)
  the two profiles are of different devices: /device:TPU:0 before, /device:TPU:27 now
where the time goes in v1:
time: 330 us; the launch traced here: 323 us
  Pallas kernels  145 us (44%)
  waiting for transfers between devices  80.6 us (24%)
  local copies, waits for them, and re-layouts  44.8 us (14%)
  starting transfers between devices  39 us (12%)
  other arithmetic  11.9 us (4%)
    pallas_call x6, Pallas kernels, attend(): pl.pallas_call(functools.partial(attend_kernel, group, backs, part, first...  93.8 us
    ppermute x10, waiting for transfers between devices, cp_shift(): lax.ppermute(array, 'cp', [(i, i + shift) for i in range(n_cp - shift)])  45.9 us
    unnamed x36, local copies, waits for them, and re-layouts  41.4 us
    pallas_call x6, Pallas kernels, product(): pl.pallas_call(functools.partial(product_kernel, block, bool(turns)), in_...  34 us
    ppermute x8, waiting for transfers between devices, sublayer(): far[back].append(lax.ppermute(here, 'cp', cross if back else own_cross))  20.6 us
    pallas_call x2, Pallas kernels, project_keys(): pl.pallas_call(functools.partial(key_value_kernel, n_tp, block), in_specs...  17.2 us
    ppermute x8, starting transfers between devices, sublayer(): far[back].append(lax.ppermute(here, 'cp', cross if back else own_cross))  14.6 us
    ppermute x4, waiting for transfers between devices, tp_shift(): lax.ppermute(array, 'tp', [(i, (i + shift) % n_tp) for i in range(n_tp)])  14.2 us
  transfers between devices with their start and end apart: 26, of which 11 were waited for; matrix products, arithmetic and copies ran while one was open for 4% of the time, Pallas kernels for 43%

profile of v1, /device:TPU:27, one launch (start us, length us, event | category | flops | bytes accessed | tf_op | source)
XLA Modules:
  0.0 323.4 jit_solution(11797113533227170614)
XLA Ops:
  7.9 4.6 %collective-permute-done.1 = s32[128]{0:T(128)S(1)} collective-permute-done((s32[128]{0:T(128)S(1)}, s32[128]{0:T(128)S(1)}, u32[]{:S(2)}, u32[]{:S(2)}) %collective-permute-start.1) | collective-permute-done | bytes 544 | tf_op jit(solution)/shard_map/ppermute | solution.py:397
  32.5 8.8 %project_keys.2 = (bf16[4,256,256]{2,1,0:T(8,128)(2,1)S(1)}, bf16[256,4096]{1,0:T(8,128)(2,1)S(1)}) custom-call(s32[16]{0:T(128)S(1)} %compare_select_fusion.13.info, bf16[256,2048]{1,0:T(8,128)(2,1)S(1)} %get-tuple-element.29.refs_0_, bf16[256,2048]{1,0:T(8,128)(2,1)} %collective-permute-done.4.refs_1_, f32[1,4096]{1,0:T(1,128)S(1)} %bitcast.24, ...), custom_call_target="tpu_custom_call" | custom-call | flops 2147483648 | bytes 8388608 | tf_op jit(solution)/shard_map/project_keys/pallas_call | solution.py:93
  42.8 7.2 %collective-permute-done.7.refs_1_ = bf16[256,2048]{1,0:T(8,128)(2,1)} collective-permute-done((bf16[256,2048]{1,0:T(8,128)(2,1)S(1)}, bf16[256,2048]{1,0:T(8,128)(2,1)}, u32[]{:S(2)}, u32[]{:S(2)}) %collective-permute-start.7) | collective-permute-done | bytes 1048608 | tf_op jit(solution)/shard_map/ppermute | solution.py:394
  50.0 8.5 %project_keys.3 = (bf16[4,256,256]{2,1,0:T(8,128)(2,1)S(1)}, bf16[256,4096]{1,0:T(8,128)(2,1)S(1)}) custom-call(s32[16]{0:T(128)S(1)} %compare_select_fusion.13.info, bf16[256,2048]{1,0:T(8,128)(2,1)S(1)} %get-tuple-element.30.refs_0_, bf16[256,2048]{1,0:T(8,128)(2,1)} %collective-permute-done.7.refs_1_, f32[1,4096]{1,0:T(1,128)S(1)} %bitcast.25, ...), custom_call_target="tpu_custom_call" | custom-call | flops 2147483648 | bytes 8388608 | tf_op jit(solution)/shard_map/project_keys/pallas_call | solution.py:93
  62.4 12.1 %collective-permute-done.22 = bf16[4,256,256]{2,1,0:T(8,128)(2,1)S(1)} collective-permute-done((bf16[4,256,256]{2,1,0:T(8,128)(2,1)S(1)}, bf16[4,256,256]{2,1,0:T(8,128)(2,1)S(1)}, u32[]{:S(2)}, u32[]{:S(2)}) %collective-permute-start.22) | collective-permute-done | bytes 524320 | tf_op jit(solution)/shard_map/ppermute | solution.py:454
  79.0 18.4 %collective-permute-done.5 = bf16[4,256,256]{2,1,0:T(8,128)(2,1)S(1)} collective-permute-done((bf16[4,256,256]{2,1,0:T(8,128)(2,1)S(1)}, bf16[4,256,256]{2,1,0:T(8,128)(2,1)S(1)}, u32[]{:S(2)}, u32[]{:S(2)}) %collective-permute-start.5) | collective-permute-done | bytes 524320 | tf_op jit(solution)/shard_map/ppermute | solution.py:397
  101.1 7.6 %collective-permute-done.8 = bf16[4,256,256]{2,1,0:T(8,128)(2,1)S(1)} collective-permute-done((bf16[4,256,256]{2,1,0:T(8,128)(2,1)S(1)}, bf16[4,256,256]{2,1,0:T(8,128)(2,1)S(1)}, u32[]{:S(2)}, u32[]{:S(2)}) %collective-permute-start.8) | collective-permute-done | bytes 524320 | tf_op jit(solution)/shard_map/ppermute | solution.py:397
  114.8 8.8 %collective-permute-done.14 = bf16[4,256,256]{2,1,0:T(8,128)(2,1)S(1)} collective-permute-done((bf16[4,256,256]{2,1,0:T(8,128)(2,1)S(1)}, bf16[4,256,256]{2,1,0:T(8,128)(2,1)S(1)}, u32[]{:S(2)}, u32[]{:S(2)}) %collective-permute-start.14) | collective-permute-done | bytes 524320 | tf_op jit(solution)/shard_map/ppermute | solution.py:397
  127.0 5.8 %copy-done.4 = bf16[4096,2048]{1,0:T(8,128)(2,1)S(1)} copy-done((bf16[4096,2048]{1,0:T(8,128)(2,1)S(1)}, bf16[4096,2048]{1,0:T(8,128)(2,1)}, u32[]{:S(2)}) %copy-start.4) | copy-done | bytes 16777240
  132.7 8.5 %project_queries.2.q_ref = bf16[256,2048]{1,0:T(8,128)(2,1)S(1)} custom-call(s32[1]{0:T(128)} %get-tuple-element.41.offset, f32[256,128]{1,0:T(8,128)S(1)} %get-tuple-element.44.refs_3_.refs_0_, f32[256,128]{1,0:T(8,128)S(1)} %get-tuple-element.31.refs_4_.refs_1_, bf16[256,4096]{1,0:T(8,128)(2,1)S(1)} %get-tuple-element.17.refs_2_, ...), custom_call_target="tpu_custom_call" | custom-call | flops 4294967296 | bytes 16777216 | tf_op jit(solution)/shard_map/project_queries/pallas_call | solution.py:157
  152.7 5.8 %copy-done.5 = bf16[4096,2048]{1,0:T(8,128)(2,1)S(1)} copy-done((bf16[4096,2048]{1,0:T(8,128)(2,1)S(1)}, bf16[4096,2048]{1,0:T(8,128)(2,1)}, u32[]{:S(2)}) %copy-start.5) | copy-done | bytes 16777240
  158.4 8.6 %project_queries.3.q_ref = bf16[256,2048]{1,0:T(8,128)(2,1)S(1)} custom-call(s32[1]{0:T(128)} %get-tuple-element.41.offset, f32[256,128]{1,0:T(8,128)S(1)} %get-tuple-element.43.refs_3_.refs_0_, f32[256,128]{1,0:T(8,128)S(1)} %get-tuple-element.32.refs_4_.refs_1_, bf16[256,4096]{1,0:T(8,128)(2,1)S(1)} %get-tuple-element.24.refs_2_, ...), custom_call_target="tpu_custom_call" | custom-call | flops 4294967296 | bytes 16777216 | tf_op jit(solution)/shard_map/project_queries/pallas_call | solution.py:157
  167.1 4.9 %collective-permute-done.11 = bf16[4,256,256]{2,1,0:T(8,128)(2,1)} collective-permute-done((bf16[4,256,256]{2,1,0:T(8,128)(2,1)S(1)}, bf16[4,256,256]{2,1,0:T(8,128)(2,1)}, u32[]{:S(2)}, u32[]{:S(2)}) %collective-permute-start.11) | collective-permute-done | bytes 524320 | tf_op jit(solution)/shard_map/ppermute | solution.py:454
  175.3 16.8 %attend.9 = (f32[4,2,128,512]{3,2,1,0:T(8,128)S(1)}, f32[4,4,512]{2,1,0:T(4,128)S(1)}) custom-call(s32[16]{0:T(128)S(1)} %compare_select_fusion.13.info, s32[8,512]{1,0:T(8,128)S(1)} %broadcast_in_dim.79.start_ref, bf16[256,2048]{1,0:T(8,128)(2,1)S(1)} %project_queries.3.q_ref, bf16[4,4,256,256]{3,2,1,0:T(8,128)(2,1)S(1)} %pad_maximum_fusion.3.refs_0_, ...), custom_call_target="tpu_custom_call" | custom-call | flops 8589934592 | bytes 8388608 | tf_op jit(solution)/shard_map/attend/pallas_call | solution.py:358
  192.1 16.8 %attend.6 = (f32[4,2,128,512]{3,2,1,0:T(8,128)S(1)}, f32[4,4,512]{2,1,0:T(4,128)S(1)}) custom-call(s32[16]{0:T(128)S(1)} %compare_select_fusion.13.info, s32[8,512]{1,0:T(8,128)S(1)} %broadcast_in_dim.79.start_ref, bf16[256,2048]{1,0:T(8,128)(2,1)S(1)} %project_queries.2.q_ref, bf16[4,4,256,256]{3,2,1,0:T(8,128)(2,1)S(1)} %pad_maximum_fusion.3.refs_0_, ...), custom_call_target="tpu_custom_call" | custom-call | flops 8589934592 | bytes 8388608 | tf_op jit(solution)/shard_map/attend/pallas_call | solution.py:358
  209.0 27.9 %attend.10 = (f32[4,2,128,512]{3,2,1,0:T(8,128)S(1)}, f32[4,4,512]{2,1,0:T(4,128)S(1)}) custom-call(s32[16]{0:T(128)S(1)} %compare_select_fusion.13.info, s32[8,512]{1,0:T(8,128)S(1)} %broadcast_in_dim.79.start_ref, bf16[256,2048]{1,0:T(8,128)(2,1)S(1)} %project_queries.3.q_ref, ...), custom_call_target="tpu_custom_call", output_to_operand_aliasing={{0}: (7, {}), {1}: (8, {})} | custom-call | flops 17179869184 | bytes 8388608 | tf_op jit(solution)/shard_map/attend/pallas_call | solution.py:358
  239.3 27.8 %attend.7 = (f32[4,2,128,512]{3,2,1,0:T(8,128)S(1)}, f32[4,4,512]{2,1,0:T(4,128)S(1)}) custom-call(s32[16]{0:T(128)S(1)} %compare_select_fusion.13.info, s32[8,512]{1,0:T(8,128)S(1)} %broadcast_in_dim.79.start_ref, bf16[256,2048]{1,0:T(8,128)(2,1)S(1)} %project_queries.2.q_ref, ...), custom_call_target="tpu_custom_call", output_to_operand_aliasing={{0}: (7, {}), {1}: (8, {})} | custom-call | flops 17179869184 | bytes 8388608 | tf_op jit(solution)/shard_map/attend/pallas_call | solution.py:358
  269.4 5.8 %copy-done = bf16[2048,4096]{1,0:T(8,128)(2,1)S(1)} copy-done((bf16[2048,4096]{1,0:T(8,128)(2,1)S(1)}, bf16[2048,4096]{1,0:T(8,128)(2,1)}, u32[]{:S(2)}) %copy-start) | copy-done | bytes 16777240
  282.8 5.8 %copy-done.1 = bf16[2048,4096]{1,0:T(8,128)(2,1)S(1)} copy-done((bf16[2048,4096]{1,0:T(8,128)(2,1)S(1)}, bf16[2048,4096]{1,0:T(8,128)(2,1)}, u32[]{:S(2)}) %copy-start.1) | copy-done | bytes 16777240
  293.5 5.8 %copy-done.2 = bf16[2048,4096]{1,0:T(8,128)(2,1)S(1)} copy-done((bf16[2048,4096]{1,0:T(8,128)(2,1)S(1)}, bf16[2048,4096]{1,0:T(8,128)(2,1)}, u32[]{:S(2)}) %copy-start.2) | copy-done | bytes 16777240
  299.2 4.5 %partial_product.6 = bf16[256,2048]{1,0:T(8,128)(2,1)S(1)} custom-call(s32[1]{0:T(128)S(6)} %mul.36.offset, bf16[256,2048]{1,0:T(8,128)(2,1)S(1)} %attend.11.refs_0_, bf16[2048,4096]{1,0:T(8,128)(2,1)S(1)} %copy-done.2), custom_call_target="tpu_custom_call" | custom-call | flops 2147483648 | bytes 8388608 | tf_op jit(solution)/shard_map/partial_product/pallas_call | solution.py:157
  303.8 5.8 %copy-done.3 = bf16[2048,4096]{1,0:T(8,128)(2,1)S(1)} copy-done((bf16[2048,4096]{1,0:T(8,128)(2,1)S(1)}, bf16[2048,4096]{1,0:T(8,128)(2,1)}, u32[]{:S(2)}) %copy-start.3) | copy-done | bytes 16777240
  309.5 4.3 %partial_product.4 = bf16[256,2048]{1,0:T(8,128)(2,1)S(1)} custom-call(s32[1]{0:T(128)S(6)} %mul.36.offset, bf16[256,2048]{1,0:T(8,128)(2,1)S(1)} %attend.8.refs_0_, bf16[2048,4096]{1,0:T(8,128)(2,1)S(1)} %copy-done.3), custom_call_target="tpu_custom_call" | custom-call | flops 2147483648 | bytes 8388608 | tf_op jit(solution)/shard_map/partial_product/pallas_call | solution.py:157
  314.2 7.0 %collective-permute-done.25 = bf16[256,2048]{1,0:T(8,128)(2,1)S(1)} collective-permute-done((bf16[256,2048]{1,0:T(8,128)(2,1)S(1)}, bf16[256,2048]{1,0:T(8,128)(2,1)S(1)}, u32[]{:S(2)}, u32[]{:S(2)}) %collective-permute-start.25) | collective-permute-done | bytes 1048608 | tf_op jit(solution)/shard_map/ppermute | solution.py:394
  (103 shorter events, 83.9 us)
Async XLA Ops:
  0.9 5.7 %collective-permute-start = (s32[128]{0:T(128)S(1)}, s32[128]{0:T(128)S(1)}, u32[]{:S(2)}, u32[]{:S(2)}) collective-permute-start(s32[128]{0:T(128)S(1)} %convert_reduce_fusion.1), channel_id=1, source_target_pairs={{0,2},{2,4},{4,6},{6,8},{8,10},{10,12},{12,14},{14,16},{16,18},{18... | collective-permute-start | bytes 1544 | tf_op jit(solution)/shard_map/ppermute | solution.py:397
  4.0 24.1 %collective-permute-start.4 = (bf16[256,2048]{1,0:T(8,128)(2,1)S(1)}, bf16[256,2048]{1,0:T(8,128)(2,1)}, u32[]{:S(2)}, u32[]{:S(2)}) collective-permute-start(bf16[256,2048]{1,0:T(8,128)(2,1)S(1)} %get-tuple-element.29.refs_0_), channel_id=1, source_target_pairs={{0,1},{1,0},{2,3},{3,2},{4,5},{5,4},{6,7},{7,6},{8,9},{9,8},{10,11... | collective-permute-start | bytes 3145736 | tf_op jit(solution)/shard_map/ppermute | solution.py:394
  5.3 44.7 %collective-permute-start.7 = (bf16[256,2048]{1,0:T(8,128)(2,1)S(1)}, bf16[256,2048]{1,0:T(8,128)(2,1)}, u32[]{:S(2)}, u32[]{:S(2)}) collective-permute-start(bf16[256,2048]{1,0:T(8,128)(2,1)S(1)} %get-tuple-element.30.refs_0_), channel_id=1, source_target_pairs={{0,1},{1,0},{2,3},{3,2},{4,5},{5,4},{6,7},{7,6},{8,9},{9,8},{10,11... | collective-permute-start | bytes 3145736 | tf_op jit(solution)/shard_map/ppermute | solution.py:394
  6.5 5.9 %collective-permute-start.1 = (s32[128]{0:T(128)S(1)}, s32[128]{0:T(128)S(1)}, u32[]{:S(2)}, u32[]{:S(2)}) collective-permute-start(s32[128]{0:T(128)S(1)} %add.43), channel_id=1, source_target_pairs={{0,4},{2,6},{4,8},{6,10},{8,12},{10,14},{12,16},{14,18},{16,20},{1... | collective-permute-start | bytes 1544 | tf_op jit(solution)/shard_map/ppermute | solution.py:397
  41.2 21.1 %collective-permute-start.21 = (bf16[4,256,256]{2,1,0:T(8,128)(2,1)S(1)}, bf16[4,256,256]{2,1,0:T(8,128)(2,1)S(1)}, u32[]{:S(2)}, u32[]{:S(2)}) collective-permute-start(bf16[4,256,256]{2,1,0:T(8,128)(2,1)S(1)} %get-tuple-element.18), channel_id=1, source_target_pairs={{0,4},{2,6},{8,12},{10,14},{16,20},{18,22},{24,28},{26,30},{1,5},{... | collective-permute-start | bytes 1572872 | tf_op jit(solution)/shard_map/ppermute | solution.py:454
  58.5 16.0 %collective-permute-start.22 = (bf16[4,256,256]{2,1,0:T(8,128)(2,1)S(1)}, bf16[4,256,256]{2,1,0:T(8,128)(2,1)S(1)}, u32[]{:S(2)}, u32[]{:S(2)}) collective-permute-start(bf16[4,256,256]{2,1,0:T(8,128)(2,1)S(1)} %get-tuple-element.19), channel_id=1, source_target_pairs={{0,4},{2,6},{8,12},{10,14},{16,20},{18,22},{24,28},{26,30},{1,5},{... | collective-permute-start | bytes 1572872 | tf_op jit(solution)/shard_map/ppermute | solution.py:454
  59.8 37.6 %collective-permute-start.5 = (bf16[4,256,256]{2,1,0:T(8,128)(2,1)S(1)}, bf16[4,256,256]{2,1,0:T(8,128)(2,1)S(1)}, u32[]{:S(2)}, u32[]{:S(2)}) collective-permute-start(bf16[4,256,256]{2,1,0:T(8,128)(2,1)S(1)} %get-tuple-element.18), channel_id=1, source_target_pairs={{0,16},{2,18},{4,20},{6,22},{8,24},{10,26},{12,28},{14,30},{1,17},... | collective-permute-start | bytes 1572872 | tf_op jit(solution)/shard_map/ppermute | solution.py:397
  61.1 47.6 %collective-permute-start.8 = (bf16[4,256,256]{2,1,0:T(8,128)(2,1)S(1)}, bf16[4,256,256]{2,1,0:T(8,128)(2,1)S(1)}, u32[]{:S(2)}, u32[]{:S(2)}) collective-permute-start(bf16[4,256,256]{2,1,0:T(8,128)(2,1)S(1)} %get-tuple-element.19), channel_id=1, source_target_pairs={{0,16},{2,18},{4,20},{6,22},{8,24},{10,26},{12,28},{14,30},{1,17},... | collective-permute-start | bytes 1572872 | tf_op jit(solution)/shard_map/ppermute | solution.py:397
  74.8 100.5 %collective-permute-start.23 = (bf16[4,4,256,256]{3,2,1,0:T(8,128)(2,1)S(1)}, bf16[4,4,256,256]{3,2,1,0:T(8,128)(2,1)}, u32[]{:S(2)}, u32[]{:S(2)}) collective-permute-start(bf16[4,4,256,256]{3,2,1,0:T(8,128)(2,1)S(1)} %pad_maximum_fusion.3.refs_0_), channel_id=1, source_target_pairs={{0,2},{2,0},{4,6},{6,4},{8,10},{10,8},{12,14},{14,12},{16,18},{18,... | collective-permute-start | bytes 6291464 | tf_op jit(solution)/shard_map/ppermute | solution.py:462
  76.5 37.0 %collective-permute-start.13 = (bf16[4,256,256]{2,1,0:T(8,128)(2,1)S(1)}, bf16[4,256,256]{2,1,0:T(8,128)(2,1)S(1)}, u32[]{:S(2)}, u32[]{:S(2)}) collective-permute-start(bf16[4,256,256]{2,1,0:T(8,128)(2,1)S(1)} %get-tuple-element.18), channel_id=1, source_target_pairs={{0,8},{2,10},{4,12},{6,14},{8,16},{10,18},{12,20},{14,22},{16,24},... | collective-permute-start | bytes 1572872 | tf_op jit(solution)/shard_map/ppermute | solution.py:397
  77.7 45.9 %collective-permute-start.14 = (bf16[4,256,256]{2,1,0:T(8,128)(2,1)S(1)}, bf16[4,256,256]{2,1,0:T(8,128)(2,1)S(1)}, u32[]{:S(2)}, u32[]{:S(2)}) collective-permute-start(bf16[4,256,256]{2,1,0:T(8,128)(2,1)S(1)} %get-tuple-element.19), channel_id=1, source_target_pairs={{0,8},{2,10},{4,12},{6,14},{8,16},{10,18},{12,20},{14,22},{16,24},... | collective-permute-start | bytes 1572872 | tf_op jit(solution)/shard_map/ppermute | solution.py:397
  97.4 28.0 %collective-permute-start.18 = (bf16[4,256,256]{2,1,0:T(8,128)(2,1)S(1)}, bf16[4,256,256]{2,1,0:T(8,128)(2,1)S(1)}, u32[]{:S(2)}, u32[]{:S(2)}) collective-permute-start(bf16[4,256,256]{2,1,0:T(8,128)(2,1)S(1)} %collective-permute-done.5), channel_id=1, source_target_pairs={{0,4},{2,6},{4,0},{6,2},{8,12},{10,14},{12,8},{14,10},{16,20},{18,... | collective-permute-start | bytes 1572872 | tf_op jit(solution)/shard_map/ppermute | solution.py:454
  108.6 17.0 %collective-permute-start.19 = (bf16[4,256,256]{2,1,0:T(8,128)(2,1)S(1)}, bf16[4,256,256]{2,1,0:T(8,128)(2,1)S(1)}, u32[]{:S(2)}, u32[]{:S(2)}) collective-permute-start(bf16[4,256,256]{2,1,0:T(8,128)(2,1)S(1)} %collective-permute-done.8), channel_id=1, source_target_pairs={{0,4},{2,6},{4,0},{6,2},{8,12},{10,14},{12,8},{14,10},{16,20},{18,... | collective-permute-start | bytes 1572872 | tf_op jit(solution)/shard_map/ppermute | solution.py:454
  113.5 29.5 %collective-permute-start.6 = (bf16[4,256,256]{2,1,0:T(8,128)(2,1)S(1)}, bf16[4,256,256]{2,1,0:T(8,128)(2,1)S(1)}, u32[]{:S(2)}, u32[]{:S(2)}) collective-permute-start(bf16[4,256,256]{2,1,0:T(8,128)(2,1)S(1)} %collective-permute-done.5), channel_id=1, source_target_pairs={{0,8},{2,10},{4,12},{6,14},{8,16},{10,18},{12,20},{14,22},{16,24},... | collective-permute-start | bytes 1572872 | tf_op jit(solution)/shard_map/ppermute | solution.py:397
  123.6 19.4 %collective-permute-start.9 = (bf16[4,256,256]{2,1,0:T(8,128)(2,1)S(1)}, bf16[4,256,256]{2,1,0:T(8,128)(2,1)S(1)}, u32[]{:S(2)}, u32[]{:S(2)}) collective-permute-start(bf16[4,256,256]{2,1,0:T(8,128)(2,1)S(1)} %collective-permute-done.8), channel_id=1, source_target_pairs={{0,8},{2,10},{4,12},{6,14},{8,16},{10,18},{12,20},{14,22},{16,24},... | collective-permute-start | bytes 1572872 | tf_op jit(solution)/shard_map/ppermute | solution.py:397
  125.4 16.1 %collective-permute-start.15 = (bf16[4,256,256]{2,1,0:T(8,128)(2,1)S(1)}, bf16[4,256,256]{2,1,0:T(8,128)(2,1)S(1)}, u32[]{:S(2)}, u32[]{:S(2)}) collective-permute-start(bf16[4,256,256]{2,1,0:T(8,128)(2,1)S(1)} %collective-permute-done.13), channel_id=1, source_target_pairs={{0,4},{2,6},{4,0},{6,2},{8,12},{10,14},{12,8},{14,10},{16,20},{18,... | collective-permute-start | bytes 1572872 | tf_op jit(solution)/shard_map/ppermute | solution.py:454
  125.7 23.7 %collective-permute-start.16 = (bf16[4,256,256]{2,1,0:T(8,128)(2,1)S(1)}, bf16[4,256,256]{2,1,0:T(8,128)(2,1)S(1)}, u32[]{:S(2)}, u32[]{:S(2)}) collective-permute-start(bf16[4,256,256]{2,1,0:T(8,128)(2,1)S(1)} %collective-permute-done.14), channel_id=1, source_target_pairs={{0,4},{2,6},{4,0},{6,2},{8,12},{10,14},{12,8},{14,10},{16,20},{18,... | collective-permute-start | bytes 1572872 | tf_op jit(solution)/shard_map/ppermute | solution.py:454
  141.6 67.4 %collective-permute-start.20 = (bf16[4,4,256,256]{3,2,1,0:T(8,128)(2,1)S(1)}, bf16[4,4,256,256]{3,2,1,0:T(8,128)(2,1)S(1)}, u32[]{:S(2)}, u32[]{:S(2)}) collective-permute-start(bf16[4,4,256,256]{3,2,1,0:T(8,128)(2,1)S(1)} %pad_maximum_fusion.2.refs_2_), channel_id=1, source_target_pairs={{0,2},{2,0},{4,6},{6,4},{8,10},{10,8},{12,14},{14,12},{16,18},{18,... | collective-permute-start | bytes 6291464 | tf_op jit(solution)/shard_map/ppermute | solution.py:462
  143.0 24.1 %collective-permute-start.10 = (bf16[4,256,256]{2,1,0:T(8,128)(2,1)S(1)}, bf16[4,256,256]{2,1,0:T(8,128)(2,1)}, u32[]{:S(2)}, u32[]{:S(2)}) collective-permute-start(bf16[4,256,256]{2,1,0:T(8,128)(2,1)S(1)} %collective-permute-done.6), channel_id=1, source_target_pairs={{0,4},{2,6},{4,0},{6,2},{8,12},{10,14},{12,8},{14,10},{16,20},{18,... | collective-permute-start | bytes 1572872 | tf_op jit(solution)/shard_map/ppermute | solution.py:454
  143.0 28.9 %collective-permute-start.11 = (bf16[4,256,256]{2,1,0:T(8,128)(2,1)S(1)}, bf16[4,256,256]{2,1,0:T(8,128)(2,1)}, u32[]{:S(2)}, u32[]{:S(2)}) collective-permute-start(bf16[4,256,256]{2,1,0:T(8,128)(2,1)S(1)} %collective-permute-done.9), channel_id=1, source_target_pairs={{0,4},{2,6},{4,0},{6,2},{8,12},{10,14},{12,8},{14,10},{16,20},{18,... | collective-permute-start | bytes 1572872 | tf_op jit(solution)/shard_map/ppermute | solution.py:454
  149.7 59.3 %collective-permute-start.17 = (bf16[4,4,256,256]{3,2,1,0:T(8,128)(2,1)S(1)}, bf16[4,4,256,256]{3,2,1,0:T(8,128)(2,1)}, u32[]{:S(2)}, u32[]{:S(2)}) collective-permute-start(bf16[4,4,256,256]{3,2,1,0:T(8,128)(2,1)S(1)} %pad_maximum_fusion.1.refs_0_), channel_id=1, source_target_pairs={{0,2},{2,0},{4,6},{6,4},{8,10},{10,8},{12,14},{14,12},{16,18},{18,... | collective-permute-start | bytes 6291464 | tf_op jit(solution)/shard_map/ppermute | solution.py:462
  173.6 93.5 %collective-permute-start.12 = (bf16[4,4,256,256]{3,2,1,0:T(8,128)(2,1)S(1)}, bf16[4,4,256,256]{3,2,1,0:T(8,128)(2,1)S(1)}, u32[]{:S(2)}, u32[]{:S(2)}) collective-permute-start(bf16[4,4,256,256]{3,2,1,0:T(8,128)(2,1)S(1)} %pad_maximum_fusion.refs_0_), channel_id=1, source_target_pairs={{0,2},{2,0},{4,6},{6,4},{8,10},{10,8},{12,14},{14,12},{16,18},{18,... | collective-permute-start | bytes 6291464 | tf_op jit(solution)/shard_map/ppermute | solution.py:462
  279.2 34.6 %collective-permute-start.24 = (bf16[256,2048]{1,0:T(8,128)(2,1)S(1)}, bf16[256,2048]{1,0:T(8,128)(2,1)S(1)}, u32[]{:S(2)}, u32[]{:S(2)}) collective-permute-start(bf16[256,2048]{1,0:T(8,128)(2,1)S(1)} %partial_product.5), channel_id=1, source_target_pairs={{0,1},{1,0},{2,3},{3,2},{4,5},{5,4},{6,7},{7,6},{8,9},{9,8},{10,11... | collective-permute-start | bytes 3145736 | tf_op jit(solution)/shard_map/ppermute | solution.py:394
  292.6 28.6 %collective-permute-start.25 = (bf16[256,2048]{1,0:T(8,128)(2,1)S(1)}, bf16[256,2048]{1,0:T(8,128)(2,1)S(1)}, u32[]{:S(2)}, u32[]{:S(2)}) collective-permute-start(bf16[256,2048]{1,0:T(8,128)(2,1)S(1)} %partial_product.7), channel_id=1, source_target_pairs={{0,1},{1,0},{2,3},{3,2},{4,5},{5,4},{6,7},{7,6},{8,9},{9,8},{10,11... | collective-permute-start | bytes 3145736 | tf_op jit(solution)/shard_map/ppermute | solution.py:394
  (20 other events, 216.7 us)

commit v2 on v1

--- a/solution.py
+++ b/solution.py
@@ -15,7 +15,7 @@
 MASKED = -1e30
 LOG2E = 1.4426950408889634
 PLANE = 4
-VMEM = 32 * 1024 * 1024
+ALONE = 52 * 1024 * 1024
 GRANT = 24 * 1024 * 1024
 
 
@@ -88,7 +88,7 @@
     depth, columns = w_key.shape
     block = min(2 * HEAD_SIZE, columns)
     steps = columns // block
-    away = pl.BlockSpec(memory_space=pl.ANY)
+    away = pl.BlockSpec(memory_space=pltpu.HBM)
     near = pl.BlockSpec(memory_space=pltpu.VMEM)
     return pl.pallas_call(
         functools.partial(key_value_kernel, n_tp, block),
@@ -109,7 +109,7 @@
             pltpu.SemaphoreType.DMA((2 * steps,)),
             pltpu.SemaphoreType.DMA,
         ],
-        compiler_params=pltpu.CompilerParams(vmem_limit_bytes=VMEM),
+        compiler_params=pltpu.CompilerParams(vmem_limit_bytes=ALONE),
         cost_estimate=pl.CostEstimate(
             flops=4 * tokens * depth * columns, bytes_accessed=4 * depth * columns, transcendentals=0
         ),
@@ -117,11 +117,13 @@
     )(info, *pieces, gain, cosine, sine, w_key, w_value)
 
 
-def product_kernel(block, rotary, offset, *refs):
+def product_kernel(block, parts, rotary, offset, *refs):
     if rotary:
         cos_ref, sin_ref, refs = refs[0], refs[1], refs[2:]
-    x_hbm, weight_hbm, out_ref, x_ref, held, x_sem, weight_sem = refs
-    steps = out_ref.shape[1] // block
+    x_hbm, weight_hbm, out_refs = refs[:parts], refs[parts], refs[parts + 1 : 2 * parts + 1]
+    x_ref, held, x_sem, weight_sem = refs[2 * parts + 1 :]
+    rows = out_refs[0].shape[0]
+    steps = out_refs[0].shape[1] // block
 
     def copy(step):
         columns = pl.ds(pl.multiple_of(offset[0] + step * block, HEAD_SIZE), block)
@@ -129,11 +131,16 @@
             weight_hbm.at[:, columns], held.at[step], weight_sem.at[step]
         )
 
-    x_copy = pltpu.make_async_copy(x_hbm, x_ref, x_sem)
-    x_copy.start()
+    x_copies = [
+        pltpu.make_async_copy(x, x_ref.at[pl.ds(i * rows, rows)], x_sem.at[i])
+        for i, x in enumerate(x_hbm)
+    ]
+    for x_copy in x_copies:
+        x_copy.start()
     for step in range(steps):
         copy(step).start()
-    x_copy.wait()
+    for x_copy in x_copies:
+        x_copy.wait()
 
     def body(step, _):
         copy(step).wait()
@@ -141,46 +148,69 @@
         columns = pl.ds(pl.multiple_of(step * block, block), block)
         if rotary:
             result = jnp.concatenate(turn(result, cos_ref[...], sin_ref[...]), axis=1)
-        out_ref[:, columns] = result.astype(jnp.bfloat16)
+        result = result.astype(jnp.bfloat16)
+        for i, out_ref in enumerate(out_refs):
+            out_ref[:, columns] = result[i * rows : (i + 1) * rows]
         return 0
 
     lax.fori_loop(0, steps, body, 0)
 
 
-def product(x, weights, offset, columns, turns=None):
-    tokens, depth = x.shape
+def product(xs, weights, offset, columns, turns=()):
+    rows, depth = xs[0].shape
+    tokens = rows * len(xs)
     block = min(4 * HEAD_SIZE, columns)
     steps = columns // block
-    away = pl.BlockSpec(memory_space=pl.ANY)
+    away = pl.BlockSpec(memory_space=pltpu.HBM)
     near = pl.BlockSpec(memory_space=pltpu.VMEM)
-    turns = turns or ()
     return pl.pallas_call(
-        functools.partial(product_kernel, block, bool(turns)),
-        in_specs=[pl.BlockSpec(memory_space=pltpu.SMEM)] + [near] * len(turns) + [away, away],
-        out_specs=near,
-        out_shape=jax.ShapeDtypeStruct((tokens, columns), jnp.bfloat16),
+        functools.partial(product_kernel, block, len(xs), bool(turns)),
+        in_specs=[pl.BlockSpec(memory_space=pltpu.SMEM)]
+        + [near] * len(turns)
+        + [away] * (len(xs) + 1),
+        out_specs=[near] * len(xs),
+        out_shape=[jax.ShapeDtypeStruct((rows, columns), jnp.bfloat16)] * len(xs),
         scratch_shapes=[
             pltpu.VMEM((tokens, depth), jnp.bfloat16),
             pltpu.VMEM((steps, depth, block), jnp.bfloat16),
-            pltpu.SemaphoreType.DMA,
+            pltpu.SemaphoreType.DMA((len(xs),)),
             pltpu.SemaphoreType.DMA((steps,)),
         ],
-        compiler_params=pltpu.CompilerParams(vmem_limit_bytes=VMEM),
+        compiler_params=pltpu.CompilerParams(vmem_limit_bytes=ALONE),
         cost_estimate=pl.CostEstimate(
             flops=2 * tokens * depth * columns,
             bytes_accessed=2 * depth * columns,
             transcendentals=0,
         ),
         name="project_queries" if turns else "partial_product",
-    )(offset, *turns, x, weights)
-
-
-def attend_kernel(group, backs, part, first, last, info, start_ref, q_ref, *refs):
+    )(offset, *turns, *xs, weights)
+
+
+def attend_kernel(group, backs, part, first, last, n_tp, info, start_ref, q_ref, *refs):
     sets, refs = refs[: 2 * len(backs)], refs[2 * len(backs) :]
     if not first:
         acc_in, stat_in, refs = refs[0], refs[1], refs[2:]
     if last:
-        out_ref, refs = refs[0], refs[1:]
+        out_hbm, out_ref, product_refs, refs = refs[0], refs[1], refs[2 : n_tp + 1], refs[n_tp + 1 :]
+        attended, held, weight_sem, refs = refs[0], refs[1], refs[2], refs[3:]
+        steps, _, block = held.shape
+        features = block * steps // (n_tp - 1) if n_tp > 1 else 0
+
+        def weight_copy(step):
+            shift = 1 + lax.div(step * block, features)
+            owner = lax.rem(info[10] + shift, n_tp)
+            low = owner * features + lax.rem(step * block, features)
+            return pltpu.make_async_copy(
+                out_hbm.at[:, pl.ds(pl.multiple_of(low, HEAD_SIZE), block)],
+                held.at[step],
+                weight_sem.at[step],
+            )
+
+        @pl.when(pl.program_id(0) == 0)
+        def _():
+            for step in range(steps):
+                weight_copy(step).start()
+
     acc, stat, rows, key_rows, value_cols, bias, score_a, score_b, units = refs
     scale = HEAD_SIZE**-0.5 * LOG2E
     queries = q_ref.shape[0]
@@ -210,8 +240,8 @@
         for array in range(2):
             for half in range(2):
                 unit = 4 * at + 2 * array + half
-                block = (layer - back) * PLANE + (inner ^ (array + 2 * half))
-                key_low = block * size
+                key_block = (layer - back) * PLANE + (inner ^ (array + 2 * half))
+                key_low = key_block * size
                 key_high = key_low + size - 1
                 need = (layer >= back) & (key_low <= query_high) & (key_high >= low_start)
                 plain = need & (key_high <= query_low) & (key_low >= high_start)
@@ -306,9 +336,29 @@
                 out_ref[:, head * HEAD_SIZE : (head + 1) * HEAD_SIZE] = done[
                     :, side * queries : (side + 1) * queries
                 ].T.astype(jnp.bfloat16)
-
-
-def attend(info, start, queries, sets, backs, part, state, local_kv, last):
+        width = group * HEAD_SIZE
+        mine = pl.ds(pl.multiple_of(pl.program_id(0) * width, width), width)
+        attended[:, mine] = out_ref[...]
+
+        @pl.when(pl.program_id(0) == pl.num_programs(0) - 1)
+        def _():
+            each = steps // len(product_refs)
+            for at, product_ref in enumerate(product_refs):
+
+                def multiply(index, _):
+                    step = at * each + index
+                    weight_copy(step).wait()
+                    columns = pl.ds(pl.multiple_of(index * block, block), block)
+                    product_ref[:, columns] = jnp.dot(
+                        attended[...], held[step], preferred_element_type=jnp.float32
+                    ).astype(jnp.bfloat16)
+                    return 0
+
+                lax.fori_loop(0, each, multiply, 0)
+
+
+def attend(info, start, queries, sets, backs, part, state, local_kv, w_out, n_tp):
+    last = w_out is not None
     tokens, columns = queries.shape
     group = columns // HEAD_SIZE // local_kv
     tiles = group // 2
@@ -343,9 +393,19 @@
         if not last:
             aliases = {len(operands) - 2: 0, len(operands) - 1: 1}
     if last:
-        out_specs = [q_block]
+        depth, width = w_out.shape
+        features = width // n_tp
+        block = min(4 * HEAD_SIZE, features)
+        steps = (n_tp - 1) * features // block
+        in_specs += [pl.BlockSpec(memory_space=pltpu.HBM)]
+        operands += [w_out]
+        out_specs = [q_block] + [pl.BlockSpec((tokens, features), lambda g, s: (0, 0))] * (n_tp - 1)
         out_shape = [jax.ShapeDtypeStruct(queries.shape, jnp.bfloat16)]
+        out_shape += [jax.ShapeDtypeStruct((tokens, features), jnp.bfloat16)] * (n_tp - 1)
         scratch = [
+            pltpu.VMEM((tokens, depth), jnp.bfloat16),
+            pltpu.VMEM((steps, depth, block), jnp.bfloat16),
+            pltpu.SemaphoreType.DMA((steps,)),
             pltpu.VMEM(acc_shape, jnp.float32),
             pltpu.VMEM(stat_shape, jnp.float32),
         ] + scratch
@@ -356,7 +416,7 @@
             jax.ShapeDtypeStruct((local_kv, *stat_shape[1:]), jnp.float32),
         ]
     return pl.pallas_call(
-        functools.partial(attend_kernel, group, backs, part, first, last),
+        functools.partial(attend_kernel, group, backs, part, first, last, n_tp),
         grid_spec=pltpu.PrefetchScalarGridSpec(
             num_scalar_prefetch=1,
             grid=(local_kv,),
@@ -367,7 +427,7 @@
         out_shape=out_shape,
         input_output_aliases=aliases,
         compiler_params=pltpu.CompilerParams(
-            dimension_semantics=("arbitrary",), vmem_limit_bytes=GRANT
+            dimension_semantics=("arbitrary",), vmem_limit_bytes=ALONE if last else GRANT
         ),
         cost_estimate=pl.CostEstimate(
             flops=8 * columns * tokens * size * count,
@@ -379,7 +439,8 @@
 
 
 def set_groups(layers):
-    return [(0,)] + ([(1, 2)] if layers > 2 else []) + [(back,) for back in range(3, layers)]
+    first = [(back,) for back in range(min(2, layers))]
+    return first + [tuple(range(back, min(back + 2, layers))) for back in range(2, layers, 2)]
 
 
 def sublayer(n_cp, n_tp, parts, hidden, norm_gain, w_query, w_key, w_value, w_out, doc_ids):
@@ -435,7 +496,7 @@
 
     near = [[] for _ in range(layers)]
     far = [[] for _ in range(layers)]
-    q_parts = []
+    normed_parts = []
     cross = [(i, i ^ 2) for i in range(n_cp)]
     own_cross = [(i, i ^ 2) for i in range(n_cp) if not i & 2]
     for part in range(parts):
@@ -446,15 +507,12 @@
         for back in range(layers):
             if back == 0:
                 here = block
-            elif back <= 2:
-                here = cp_shift(block, back * PLANE)
             else:
                 here = cp_shift(near[back - 1][part], PLANE)
             near[back].append(here)
             far[back].append(lax.ppermute(here, "cp", cross if back else own_cross))
-        q_parts.append(
-            product(normed, w_query, info[15:], w_query.shape[1], (cosine[cut], sine[cut]))
-        )
+        normed_parts.append(normed)
+    q_parts = product(normed_parts, w_query, info[15:], w_query.shape[1], (cosine, sine))
     sets = []
     swap = [(i, i ^ 1) for i in range(n_cp)]
     for back in range(layers):
@@ -466,19 +524,14 @@
         for part in range(parts):
             states[part] = attend(
                 info, start_rows, q_parts[part], [sets[back] for back in backs], backs, part,
-                states[part], local_kv, backs[-1] == layers - 1,
+                states[part], local_kv, w_out if backs[-1] == layers - 1 else None, n_tp,
             )
 
     outs = []
     for part in range(parts):
-        attended = states[part][0]
-        received = []
-        for shift in range(1, n_tp):
-            owner = lax.rem(info[10:11] + shift, n_tp)
-            received.append(
-                tp_shift(product(attended, w_out, owner * features, features), shift)
-            )
-        own = product(attended, w_out, info[10:11] * features, features)
+        attended, *partials = states[part]
+        received = [tp_shift(partial, shift + 1) for shift, partial in enumerate(partials)]
+        own = product([attended], w_out, info[10:11] * features, features)[0]
         mixed = own.astype(jnp.float32)
         for other in received:
             mixed = mixed + other.astype(jnp.float32)

time: 330 us -> 297 us (0.900); the launches traced: 323 us -> 296 us
  local copies, waits for them, and re-layouts: 44.8 us -> 12 us
  Pallas kernels: 145 us -> 156 us
  starting transfers between devices: 39 us -> 33.1 us
    unnamed x36 -> x28, local copies, waits for them, and re-layouts: 41.4 us -> 8.39 us
    pallas_call x6, Pallas kernels: 93.8 us -> 106 us  [attend(): pl.pallas_call(functools.partial(attend_kernel, group, backs, part, first...]
    ppermute x10, waiting for transfers between devices: 45.9 us -> 35.6 us  [cp_shift(): lax.ppermute(array, 'cp', [(i, i + shift) for i in range(n_cp - shift)])]
    ppermute x8, waiting for transfers between devices: 20.6 us -> 28.7 us  [sublayer(): far[back].append(lax.ppermute(here, 'cp', cross if back else own_cross))]
    ppermute x8, starting transfers between devices: 14.6 us -> 10.1 us  [sublayer(): far[back].append(lax.ppermute(here, 'cp', cross if back else own_cross))]
    pallas_call x6 -> x3, Pallas kernels: 34 us -> 29.9 us  [product(): pl.pallas_call(functools.partial(product_kernel, block, len(xs), bool(tur...]
  transfers between devices with their start and end apart: 26 -> 26, of which waited for: 11 -> 11; matrix products, arithmetic and copies ran while one was open for 4% -> 5% of each run, Pallas kernels for 43% -> 45%
where the time goes in v2:
time: 297 us; the launch traced here: 296 us
  Pallas kernels  156 us (53%)
  waiting for transfers between devices  80.9 us (27%)
  starting transfers between devices  33.1 us (11%)
  other arithmetic  13.2 us (4%)
  local copies, waits for them, and re-layouts  12 us (4%)
    pallas_call x6, Pallas kernels, attend(): pl.pallas_call(functools.partial(attend_kernel, group, backs, part, first...  106 us
    ppermute x10, waiting for transfers between devices, cp_shift(): lax.ppermute(array, 'cp', [(i, i + shift) for i in range(n_cp - shift)])  35.6 us
    pallas_call x3, Pallas kernels, product(): pl.pallas_call(functools.partial(product_kernel, block, len(xs), bool(tur...  29.9 us
    ppermute x8, waiting for transfers between devices, sublayer(): far[back].append(lax.ppermute(here, 'cp', cross if back else own_cross))  28.7 us
    pallas_call x2, Pallas kernels, project_keys(): pl.pallas_call(functools.partial(key_value_kernel, n_tp, block), in_specs...  20.3 us
    ppermute x4, waiting for transfers between devices, tp_shift(): lax.ppermute(array, 'tp', [(i, (i + shift) % n_tp) for i in range(n_tp)])  16.6 us
    ppermute x10, starting transfers between devices, cp_shift(): lax.ppermute(array, 'cp', [(i, i + shift) for i in range(n_cp - shift)])  13.2 us
    ppermute x8, starting transfers between devices, sublayer(): far[back].append(lax.ppermute(here, 'cp', cross if back else own_cross))  10.1 us
  transfers between devices with their start and end apart: 26, of which 11 were waited for; matrix products, arithmetic and copies ran while one was open for 5% of the time, Pallas kernels for 45%

profile of v2, /device:TPU:27, one launch (start us, length us, event | category | flops | bytes accessed | tf_op | source)
XLA Modules:
  0.0 296.1 jit_solution(9343281623801300665)
XLA Ops:
  7.7 4.1 %collective-permute-done.1 = s32[128]{0:T(128)S(1)} collective-permute-done((s32[128]{0:T(128)S(1)}, s32[128]{0:T(128)S(1)}, u32[]{:S(2)}, u32[]{:S(2)}) %collective-permute-start.1) | collective-permute-done | bytes 544 | tf_op jit(solution)/shard_map/ppermute | solution.py:458
  13.1 3.4 %collective-permute-done.2 = s32[128]{0:T(128)S(1)} collective-permute-done((s32[128]{0:T(128)S(1)}, s32[128]{0:T(128)S(1)}, u32[]{:S(2)}, u32[]{:S(2)}) %collective-permute-start.2) | collective-permute-done | bytes 544 | tf_op jit(solution)/shard_map/ppermute | solution.py:458
  17.8 3.9 %collective-permute-done.3 = s32[128]{0:T(128)S(1)} collective-permute-done((s32[128]{0:T(128)S(1)}, s32[128]{0:T(128)S(1)}, u32[]{:S(2)}, u32[]{:S(2)}) %collective-permute-start.3) | collective-permute-done | bytes 544 | tf_op jit(solution)/shard_map/ppermute | solution.py:458
  24.8 2.5 compare_select_fusion.13.info
  28.3 10.2 %project_keys.3 = (bf16[4,256,256]{2,1,0:T(8,128)(2,1)S(1)}, bf16[256,4096]{1,0:T(8,128)(2,1)}) custom-call(s32[16]{0:T(128)S(1)} %compare_select_fusion.13.info, bf16[256,2048]{1,0:T(8,128)(2,1)S(1)} %get-tuple-element.41.refs_0_, bf16[256,2048]{1,0:T(8,128)(2,1)} %collective-permute-done.5.refs_1_, f32[1,4096]{1,0:T(1,128)S(1)} %bitcast.24, ...), custom_call_target="tpu_custom_call" | custom-call | flops 2147483648 | bytes 8388608 | tf_op jit(solution)/shard_map/project_keys/pallas_call | solution.py:93
  39.8 10.3 %collective-permute-done.4.refs_1_ = bf16[256,2048]{1,0:T(8,128)(2,1)S(1)} collective-permute-done((bf16[256,2048]{1,0:T(8,128)(2,1)S(1)}, bf16[256,2048]{1,0:T(8,128)(2,1)S(1)}, u32[]{:S(2)}, u32[]{:S(2)}) %collective-permute-start.4) | collective-permute-done | bytes 1048608 | tf_op jit(solution)/shard_map/ppermute | solution.py:455
  51.0 10.2 %project_keys.2 = (bf16[4,256,256]{2,1,0:T(8,128)(2,1)S(1)}, bf16[256,4096]{1,0:T(8,128)(2,1)}) custom-call(s32[16]{0:T(128)S(1)} %compare_select_fusion.13.info, bf16[256,2048]{1,0:T(8,128)(2,1)S(1)} %get-tuple-element.42.refs_0_, bf16[256,2048]{1,0:T(8,128)(2,1)} %copy-done.9, f32[1,4096]{1,0:T(1,128)S(1)} %bitcast.25, ...), custom_call_target="tpu_custom_call" | custom-call | flops 2147483648 | bytes 8388608 | tf_op jit(solution)/shard_map/project_keys/pallas_call | solution.py:93
  65.1 3.9 %collective-permute-start.19 = (bf16[4,256,256]{2,1,0:T(8,128)(2,1)S(1)}, bf16[4,256,256]{2,1,0:T(8,128)(2,1)S(1)}, u32[]{:S(2)}, u32[]{:S(2)}) collective-permute-start(bf16[4,256,256]{2,1,0:T(8,128)(2,1)S(1)} %collective-permute-done.8), channel_id=1, source_target_pairs={{0,4},{2,6},{4,0},{6,2},{8,12},{10,14},{12,8},{14,10},{16,20},{18,... | collective-permute-start | bytes 1572872 | tf_op jit(solution)/shard_map/ppermute | solution.py:513
  70.3 8.6 %collective-permute-done.6 = bf16[4,256,256]{2,1,0:T(8,128)(2,1)S(1)} collective-permute-done((bf16[4,256,256]{2,1,0:T(8,128)(2,1)S(1)}, bf16[4,256,256]{2,1,0:T(8,128)(2,1)S(1)}, u32[]{:S(2)}, u32[]{:S(2)}) %collective-permute-start.6) | collective-permute-done | bytes 524320 | tf_op jit(solution)/shard_map/ppermute | solution.py:458
  80.3 10.0 %collective-permute-done.21 = bf16[4,256,256]{2,1,0:T(8,128)(2,1)S(1)} collective-permute-done((bf16[4,256,256]{2,1,0:T(8,128)(2,1)S(1)}, bf16[4,256,256]{2,1,0:T(8,128)(2,1)S(1)}, u32[]{:S(2)}, u32[]{:S(2)}) %collective-permute-start.21) | collective-permute-done | bytes 524320 | tf_op jit(solution)/shard_map/ppermute | solution.py:513
  94.2 7.2 %collective-permute-done.7 = bf16[4,256,256]{2,1,0:T(8,128)(2,1)S(1)} collective-permute-done((bf16[4,256,256]{2,1,0:T(8,128)(2,1)S(1)}, bf16[4,256,256]{2,1,0:T(8,128)(2,1)S(1)}, u32[]{:S(2)}, u32[]{:S(2)}) %collective-permute-start.7) | collective-permute-done | bytes 524320 | tf_op jit(solution)/shard_map/ppermute | solution.py:458
  105.1 7.7 %collective-permute-done.18 = bf16[4,256,256]{2,1,0:T(8,128)(2,1)S(1)} collective-permute-done((bf16[4,256,256]{2,1,0:T(8,128)(2,1)S(1)}, bf16[4,256,256]{2,1,0:T(8,128)(2,1)S(1)}, u32[]{:S(2)}, u32[]{:S(2)}) %collective-permute-start.18) | collective-permute-done | bytes 524320 | tf_op jit(solution)/shard_map/ppermute | solution.py:513
  115.4 8.5 %collective-permute-done.13 = bf16[4,256,256]{2,1,0:T(8,128)(2,1)S(1)} collective-permute-done((bf16[4,256,256]{2,1,0:T(8,128)(2,1)S(1)}, bf16[4,256,256]{2,1,0:T(8,128)(2,1)S(1)}, u32[]{:S(2)}, u32[]{:S(2)}) %collective-permute-start.13) | collective-permute-done | bytes 524320 | tf_op jit(solution)/shard_map/ppermute | solution.py:458
  126.4 17.7 %project_queries.1 = (bf16[256,2048]{1,0:T(8,128)(2,1)S(1)}, bf16[256,2048]{1,0:T(8,128)(2,1)}) custom-call(s32[1]{0:T(128)} %get-tuple-element.54.offset, f32[512,128]{1,0:T(8,128)S(1)} %get-tuple-element.48.refs_0_, f32[512,128]{1,0:T(8,128)S(1)} %get-tuple-element.47.refs_1_, bf16[256,4096]{1,0:T(8,128)(2,1)} %get-tuple-element.23.refs_2_, ...), custom_call_target="tpu_custom_call" | custom-call | flops 8589934592 | bytes 16777216 | tf_op jit(solution)/shard_map/project_queries/pallas_call | solution.py:166
  146.9 10.9 %collective-permute-done.15 = bf16[4,256,256]{2,1,0:T(8,128)(2,1)} collective-permute-done((bf16[4,256,256]{2,1,0:T(8,128)(2,1)S(1)}, bf16[4,256,256]{2,1,0:T(8,128)(2,1)}, u32[]{:S(2)}, u32[]{:S(2)}) %collective-permute-start.15) | collective-permute-done | bytes 524320 | tf_op jit(solution)/shard_map/ppermute | solution.py:513
  160.7 16.3 %attend.6 = (f32[4,2,128,512]{3,2,1,0:T(8,128)S(1)}, f32[4,4,512]{2,1,0:T(4,128)S(1)}) custom-call(s32[16]{0:T(128)S(1)} %compare_select_fusion.13.info, s32[8,512]{1,0:T(8,128)S(1)} %broadcast_in_dim.79.start_ref, bf16[256,2048]{1,0:T(8,128)(2,1)S(1)} %get-tuple-element.25.q_ref, bf16[4,4,256,256]{3,2,1,0:T(8,128)(2,1)S(1)} %pad_maximum_fusion.3.refs_0_, ...), custom_call_target="tpu_custom_call" | custom-call | flops 8589934592 | bytes 8388608 | tf_op jit(solution)/shard_map/attend/pallas_call | solution.py:418
  177.1 16.4 %attend.9 = (f32[4,2,128,512]{3,2,1,0:T(8,128)S(1)}, f32[4,4,512]{2,1,0:T(4,128)S(1)}) custom-call(s32[16]{0:T(128)S(1)} %compare_select_fusion.13.info, s32[8,512]{1,0:T(8,128)S(1)} %broadcast_in_dim.79.start_ref, bf16[256,2048]{1,0:T(8,128)(2,1)S(1)} %copy-done.3, bf16[4,4,256,256]{3,2,1,0:T(8,128)(2,1)S(1)} %pad_maximum_fusion.3.refs_0_, ...), custom_call_target="tpu_custom_call" | custom-call | flops 8589934592 | bytes 8388608 | tf_op jit(solution)/shard_map/attend/pallas_call | solution.py:418
  193.5 14.9 %attend.7 = (f32[4,2,128,512]{3,2,1,0:T(8,128)S(1)}, f32[4,4,512]{2,1,0:T(4,128)S(1)}) custom-call(s32[16]{0:T(128)S(1)} %compare_select_fusion.13.info, s32[8,512]{1,0:T(8,128)S(1)} %broadcast_in_dim.79.start_ref, bf16[256,2048]{1,0:T(8,128)(2,1)S(1)} %get-tuple-element.25.q_ref, ...), custom_call_target="tpu_custom_call", output_to_operand_aliasing={{0}: (5, {}), {1}: (6, {})} | custom-call | flops 8589934592 | bytes 8388608 | tf_op jit(solution)/shard_map/attend/pallas_call | solution.py:418
  209.7 14.9 %attend.10 = (f32[4,2,128,512]{3,2,1,0:T(8,128)S(1)}, f32[4,4,512]{2,1,0:T(4,128)S(1)}) custom-call(s32[16]{0:T(128)S(1)} %compare_select_fusion.13.info, s32[8,512]{1,0:T(8,128)S(1)} %broadcast_in_dim.79.start_ref, bf16[256,2048]{1,0:T(8,128)(2,1)S(1)} %copy-done.3, ...), custom_call_target="tpu_custom_call", output_to_operand_aliasing={{0}: (5, {}), {1}: (6, {})} | custom-call | flops 8589934592 | bytes 8388608 | tf_op jit(solution)/shard_map/attend/pallas_call | solution.py:418
  228.1 21.6 %attend.8 = (bf16[256,2048]{1,0:T(8,128)(2,1)S(1)}, bf16[256,2048]{1,0:T(8,128)(2,1)}) custom-call(s32[16]{0:T(128)S(1)} %compare_select_fusion.13.info, s32[8,512]{1,0:T(8,128)S(1)} %broadcast_in_dim.79.start_ref, bf16[256,2048]{1,0:T(8,128)(2,1)} %copy-done.4, bf16[4,4,256,256]{3,2,1,0:T(8,128)(2,1)} %copy-done.7, bf16[4,4,256,256]{3,2,1,0:T(8,128)(2,1)} %copy-done.12, ...), custom_call_target="tpu_custom_call" | custom-call | flops 17179869184 | bytes 8388608 | tf_op jit(solution)/shard_map/attend/pallas_call | solution.py:418
  252.0 21.4 %attend.11 = (bf16[256,2048]{1,0:T(8,128)(2,1)S(1)}, bf16[256,2048]{1,0:T(8,128)(2,1)}) custom-call(s32[16]{0:T(128)S(1)} %compare_select_fusion.13.info, s32[8,512]{1,0:T(8,128)S(1)} %broadcast_in_dim.79.start_ref, bf16[256,2048]{1,0:T(8,128)(2,1)} %get-tuple-element.34.q_ref, bf16[4,4,256,256]{3,2,1,0:T(8,128)(2,1)} %copy-done.7, ...), custom_call_target="tpu_custom_call" | custom-call | flops 17179869184 | bytes 8388608 | tf_op jit(solution)/shard_map/attend/pallas_call | solution.py:418
  275.3 6.1 %partial_product.2 = bf16[256,2048]{1,0:T(8,128)(2,1)S(1)} custom-call(s32[1]{0:T(128)S(6)} %mul.32.offset, bf16[256,2048]{1,0:T(8,128)(2,1)} %copy-done, bf16[2048,4096]{1,0:T(8,128)(2,1)} %refs_1_.3), custom_call_target="tpu_custom_call" | custom-call | flops 2147483648 | bytes 8388608 | tf_op jit(solution)/shard_map/partial_product/pallas_call | solution.py:166
  281.3 6.1 %partial_product.3 = bf16[256,2048]{1,0:T(8,128)(2,1)S(1)} custom-call(s32[1]{0:T(128)S(6)} %mul.32.offset, bf16[256,2048]{1,0:T(8,128)(2,1)} %copy-done.1, bf16[2048,4096]{1,0:T(8,128)(2,1)} %refs_1_.3), custom_call_target="tpu_custom_call" | custom-call | flops 2147483648 | bytes 8388608 | tf_op jit(solution)/shard_map/partial_product/pallas_call | solution.py:166
  287.8 6.3 %collective-permute-done.25 = bf16[256,2048]{1,0:T(8,128)(2,1)S(1)} collective-permute-done((bf16[256,2048]{1,0:T(8,128)(2,1)}, bf16[256,2048]{1,0:T(8,128)(2,1)S(1)}, u32[]{:S(2)}, u32[]{:S(2)}) %collective-permute-start.25) | collective-permute-done | bytes 1048608 | tf_op jit(solution)/shard_map/ppermute | solution.py:455
  (91 shorter events, 51.9 us)
Async XLA Ops:
  4.1 24.2 %collective-permute-start.5 = (bf16[256,2048]{1,0:T(8,128)(2,1)S(1)}, bf16[256,2048]{1,0:T(8,128)(2,1)}, u32[]{:S(2)}, u32[]{:S(2)}) collective-permute-start(bf16[256,2048]{1,0:T(8,128)(2,1)S(1)} %get-tuple-element.41.refs_0_), channel_id=1, source_target_pairs={{0,1},{1,0},{2,3},{3,2},{4,5},{5,4},{6,7},{7,6},{8,9},{9,8},{10,11... | collective-permute-start | bytes 3145736 | tf_op jit(solution)/shard_map/ppermute | solution.py:455
  5.4 44.6 %collective-permute-start.4 = (bf16[256,2048]{1,0:T(8,128)(2,1)S(1)}, bf16[256,2048]{1,0:T(8,128)(2,1)S(1)}, u32[]{:S(2)}, u32[]{:S(2)}) collective-permute-start(bf16[256,2048]{1,0:T(8,128)(2,1)S(1)} %get-tuple-element.42.refs_0_), channel_id=1, source_target_pairs={{0,1},{1,0},{2,3},{3,2},{4,5},{5,4},{6,7},{7,6},{8,9},{9,8},{10,11... | collective-permute-start | bytes 3145736 | tf_op jit(solution)/shard_map/ppermute | solution.py:455
  5.9 5.9 %collective-permute-start.1 = (s32[128]{0:T(128)S(1)}, s32[128]{0:T(128)S(1)}, u32[]{:S(2)}, u32[]{:S(2)}) collective-permute-start(s32[128]{0:T(128)S(1)} %add.39), channel_id=1, source_target_pairs={{0,4},{2,6},{4,8},{6,10},{8,12},{10,14},{12,16},{14,18},{16,20},{1... | collective-permute-start | bytes 1544 | tf_op jit(solution)/shard_map/ppermute | solution.py:458
  16.5 5.2 %collective-permute-start.3 = (s32[128]{0:T(128)S(1)}, s32[128]{0:T(128)S(1)}, u32[]{:S(2)}, u32[]{:S(2)}) collective-permute-start(s32[128]{0:T(128)S(1)} %add.41), channel_id=1, source_target_pairs={{0,16},{2,18},{4,20},{6,22},{8,24},{10,26},{12,28},{14,30},{1,17},... | collective-permute-start | bytes 1544 | tf_op jit(solution)/shard_map/ppermute | solution.py:458
  38.5 26.6 %collective-permute-start.8 = (bf16[4,256,256]{2,1,0:T(8,128)(2,1)S(1)}, bf16[4,256,256]{2,1,0:T(8,128)(2,1)S(1)}, u32[]{:S(2)}, u32[]{:S(2)}) collective-permute-start(bf16[4,256,256]{2,1,0:T(8,128)(2,1)S(1)} %get-tuple-element.27), channel_id=1, source_target_pairs={{0,8},{2,10},{4,12},{6,14},{8,16},{10,18},{12,20},{14,22},{16,24},... | collective-permute-start | bytes 1572872 | tf_op jit(solution)/shard_map/ppermute | solution.py:458
  61.2 17.7 %collective-permute-start.6 = (bf16[4,256,256]{2,1,0:T(8,128)(2,1)S(1)}, bf16[4,256,256]{2,1,0:T(8,128)(2,1)S(1)}, u32[]{:S(2)}, u32[]{:S(2)}) collective-permute-start(bf16[4,256,256]{2,1,0:T(8,128)(2,1)S(1)} %get-tuple-element.26), channel_id=1, source_target_pairs={{0,8},{2,10},{4,12},{6,14},{8,16},{10,18},{12,20},{14,22},{16,24},... | collective-permute-start | bytes 1572872 | tf_op jit(solution)/shard_map/ppermute | solution.py:458
  62.5 17.9 %collective-permute-start.22 = (bf16[4,256,256]{2,1,0:T(8,128)(2,1)S(1)}, bf16[4,256,256]{2,1,0:T(8,128)(2,1)S(1)}, u32[]{:S(2)}, u32[]{:S(2)}) collective-permute-start(bf16[4,256,256]{2,1,0:T(8,128)(2,1)S(1)} %get-tuple-element.27), channel_id=1, source_target_pairs={{0,4},{2,6},{8,12},{10,14},{16,20},{18,22},{24,28},{26,30},{1,5},{... | collective-permute-start | bytes 1572872 | tf_op jit(solution)/shard_map/ppermute | solution.py:513
  63.8 26.6 %collective-permute-start.21 = (bf16[4,256,256]{2,1,0:T(8,128)(2,1)S(1)}, bf16[4,256,256]{2,1,0:T(8,128)(2,1)S(1)}, u32[]{:S(2)}, u32[]{:S(2)}) collective-permute-start(bf16[4,256,256]{2,1,0:T(8,128)(2,1)S(1)} %get-tuple-element.26), channel_id=1, source_target_pairs={{0,4},{2,6},{8,12},{10,14},{16,20},{18,22},{24,28},{26,30},{1,5},{... | collective-permute-start | bytes 1572872 | tf_op jit(solution)/shard_map/ppermute | solution.py:513
  65.1 37.6 %collective-permute-start.19 = (bf16[4,256,256]{2,1,0:T(8,128)(2,1)S(1)}, bf16[4,256,256]{2,1,0:T(8,128)(2,1)S(1)}, u32[]{:S(2)}, u32[]{:S(2)}) collective-permute-start(bf16[4,256,256]{2,1,0:T(8,128)(2,1)S(1)} %collective-permute-done.8), channel_id=1, source_target_pairs={{0,4},{2,6},{4,0},{6,2},{8,12},{10,14},{12,8},{14,10},{16,20},{18,... | collective-permute-start | bytes 1572872 | tf_op jit(solution)/shard_map/ppermute | solution.py:513
  69.0 23.9 %collective-permute-start.9 = (bf16[4,256,256]{2,1,0:T(8,128)(2,1)S(1)}, bf16[4,256,256]{2,1,0:T(8,128)(2,1)S(1)}, u32[]{:S(2)}, u32[]{:S(2)}) collective-permute-start(bf16[4,256,256]{2,1,0:T(8,128)(2,1)S(1)} %collective-permute-done.8), channel_id=1, source_target_pairs={{0,8},{2,10},{4,12},{6,14},{8,16},{10,18},{12,20},{14,22},{16,24},... | collective-permute-start | bytes 1572872 | tf_op jit(solution)/shard_map/ppermute | solution.py:458
  78.9 22.5 %collective-permute-start.7 = (bf16[4,256,256]{2,1,0:T(8,128)(2,1)S(1)}, bf16[4,256,256]{2,1,0:T(8,128)(2,1)S(1)}, u32[]{:S(2)}, u32[]{:S(2)}) collective-permute-start(bf16[4,256,256]{2,1,0:T(8,128)(2,1)S(1)} %collective-permute-done.6), channel_id=1, source_target_pairs={{0,8},{2,10},{4,12},{6,14},{8,16},{10,18},{12,20},{14,22},{16,24},... | collective-permute-start | bytes 1572872 | tf_op jit(solution)/shard_map/ppermute | solution.py:458
  90.6 70.1 %collective-permute-start.23 = (bf16[4,4,256,256]{3,2,1,0:T(8,128)(2,1)S(1)}, bf16[4,4,256,256]{3,2,1,0:T(8,128)(2,1)S(1)}, u32[]{:S(2)}, u32[]{:S(2)}) collective-permute-start(bf16[4,4,256,256]{3,2,1,0:T(8,128)(2,1)S(1)} %pad_maximum_fusion.3.refs_0_), channel_id=1, source_target_pairs={{0,2},{2,0},{4,6},{6,4},{8,10},{10,8},{12,14},{14,12},{16,18},{18,... | collective-permute-start | bytes 6291464 | tf_op jit(solution)/shard_map/ppermute | solution.py:520
  92.9 19.9 %collective-permute-start.18 = (bf16[4,256,256]{2,1,0:T(8,128)(2,1)S(1)}, bf16[4,256,256]{2,1,0:T(8,128)(2,1)S(1)}, u32[]{:S(2)}, u32[]{:S(2)}) collective-permute-start(bf16[4,256,256]{2,1,0:T(8,128)(2,1)S(1)} %collective-permute-done.6), channel_id=1, source_target_pairs={{0,4},{2,6},{4,0},{6,2},{8,12},{10,14},{12,8},{14,10},{16,20},{18,... | collective-permute-start | bytes 1572872 | tf_op jit(solution)/shard_map/ppermute | solution.py:513
  92.9 22.5 %collective-permute-start.14 = (bf16[4,256,256]{2,1,0:T(8,128)(2,1)S(1)}, bf16[4,256,256]{2,1,0:T(8,128)(2,1)S(1)}, u32[]{:S(2)}, u32[]{:S(2)}) collective-permute-start(bf16[4,256,256]{2,1,0:T(8,128)(2,1)S(1)} %collective-permute-done.9), channel_id=1, source_target_pairs={{0,8},{2,10},{4,12},{6,14},{8,16},{10,18},{12,20},{14,22},{16,24},... | collective-permute-start | bytes 1572872 | tf_op jit(solution)/shard_map/ppermute | solution.py:458
  101.3 22.5 %collective-permute-start.13 = (bf16[4,256,256]{2,1,0:T(8,128)(2,1)S(1)}, bf16[4,256,256]{2,1,0:T(8,128)(2,1)S(1)}, u32[]{:S(2)}, u32[]{:S(2)}) collective-permute-start(bf16[4,256,256]{2,1,0:T(8,128)(2,1)S(1)} %collective-permute-done.7), channel_id=1, source_target_pairs={{0,8},{2,10},{4,12},{6,14},{8,16},{10,18},{12,20},{14,22},{16,24},... | collective-permute-start | bytes 1572872 | tf_op jit(solution)/shard_map/ppermute | solution.py:458
  102.6 23.0 %collective-permute-start.11 = (bf16[4,256,256]{2,1,0:T(8,128)(2,1)S(1)}, bf16[4,256,256]{2,1,0:T(8,128)(2,1)S(1)}, u32[]{:S(2)}, u32[]{:S(2)}) collective-permute-start(bf16[4,256,256]{2,1,0:T(8,128)(2,1)S(1)} %collective-permute-done.9), channel_id=1, source_target_pairs={{0,4},{2,6},{4,0},{6,2},{8,12},{10,14},{12,8},{14,10},{16,20},{18,... | collective-permute-start | bytes 1572872 | tf_op jit(solution)/shard_map/ppermute | solution.py:513
  113.1 80.4 %collective-permute-start.20 = (bf16[4,4,256,256]{3,2,1,0:T(8,128)(2,1)S(1)}, bf16[4,4,256,256]{3,2,1,0:T(8,128)(2,1)S(1)}, u32[]{:S(2)}, u32[]{:S(2)}) collective-permute-start(bf16[4,4,256,256]{3,2,1,0:T(8,128)(2,1)S(1)} %pad_maximum_fusion.2.refs_0_), channel_id=1, source_target_pairs={{0,2},{2,0},{4,6},{6,4},{8,10},{10,8},{12,14},{14,12},{16,18},{18,... | collective-permute-start | bytes 6291464 | tf_op jit(solution)/shard_map/ppermute | solution.py:520
  115.4 28.8 %collective-permute-start.10 = (bf16[4,256,256]{2,1,0:T(8,128)(2,1)S(1)}, bf16[4,256,256]{2,1,0:T(8,128)(2,1)}, u32[]{:S(2)}, u32[]{:S(2)}) collective-permute-start(bf16[4,256,256]{2,1,0:T(8,128)(2,1)S(1)} %collective-permute-done.7), channel_id=1, source_target_pairs={{0,4},{2,6},{4,0},{6,2},{8,12},{10,14},{12,8},{14,10},{16,20},{18,... | collective-permute-start | bytes 1572872 | tf_op jit(solution)/shard_map/ppermute | solution.py:513
  123.8 23.1 %collective-permute-start.16 = (bf16[4,256,256]{2,1,0:T(8,128)(2,1)S(1)}, bf16[4,256,256]{2,1,0:T(8,128)(2,1)}, u32[]{:S(2)}, u32[]{:S(2)}) collective-permute-start(bf16[4,256,256]{2,1,0:T(8,128)(2,1)S(1)} %collective-permute-done.14), channel_id=1, source_target_pairs={{0,4},{2,6},{4,0},{6,2},{8,12},{10,14},{12,8},{14,10},{16,20},{18,... | collective-permute-start | bytes 1572872 | tf_op jit(solution)/shard_map/ppermute | solution.py:513
  125.6 32.2 %collective-permute-start.15 = (bf16[4,256,256]{2,1,0:T(8,128)(2,1)S(1)}, bf16[4,256,256]{2,1,0:T(8,128)(2,1)}, u32[]{:S(2)}, u32[]{:S(2)}) collective-permute-start(bf16[4,256,256]{2,1,0:T(8,128)(2,1)S(1)} %collective-permute-done.13), channel_id=1, source_target_pairs={{0,4},{2,6},{4,0},{6,2},{8,12},{10,14},{12,8},{14,10},{16,20},{18,... | collective-permute-start | bytes 1572872 | tf_op jit(solution)/shard_map/ppermute | solution.py:513
  146.0 80.1 %collective-permute-start.12 = (bf16[4,4,256,256]{3,2,1,0:T(8,128)(2,1)S(1)}, bf16[4,4,256,256]{3,2,1,0:T(8,128)(2,1)S(1)}, u32[]{:S(2)}, u32[]{:S(2)}) collective-permute-start(bf16[4,4,256,256]{3,2,1,0:T(8,128)(2,1)S(1)} %pad_maximum_fusion.refs_0_), channel_id=1, source_target_pairs={{0,2},{2,0},{4,6},{6,4},{8,10},{10,8},{12,14},{14,12},{16,18},{18,... | collective-permute-start | bytes 6291464 | tf_op jit(solution)/shard_map/ppermute | solution.py:520
  159.3 66.8 %collective-permute-start.17 = (bf16[4,4,256,256]{3,2,1,0:T(8,128)(2,1)S(1)}, bf16[4,4,256,256]{3,2,1,0:T(8,128)(2,1)S(1)}, u32[]{:S(2)}, u32[]{:S(2)}) collective-permute-start(bf16[4,4,256,256]{3,2,1,0:T(8,128)(2,1)S(1)} %pad_maximum_fusion.1.refs_2_), channel_id=1, source_target_pairs={{0,2},{2,0},{4,6},{6,4},{8,10},{10,8},{12,14},{14,12},{16,18},{18,... | collective-permute-start | bytes 6291464 | tf_op jit(solution)/shard_map/ppermute | solution.py:520
  250.8 36.7 %collective-permute-start.24 = (bf16[256,2048]{1,0:T(8,128)(2,1)}, bf16[256,2048]{1,0:T(8,128)(2,1)S(1)}, u32[]{:S(2)}, u32[]{:S(2)}) collective-permute-start(bf16[256,2048]{1,0:T(8,128)(2,1)} %get-tuple-element.33), channel_id=1, source_target_pairs={{0,1},{1,0},{2,3},{3,2},{4,5},{5,4},{6,7},{7,6},{8,9},{9,8},{10,11... | collective-permute-start | bytes 3145736 | tf_op jit(solution)/shard_map/ppermute | solution.py:455
  274.3 19.8 %collective-permute-start.25 = (bf16[256,2048]{1,0:T(8,128)(2,1)}, bf16[256,2048]{1,0:T(8,128)(2,1)S(1)}, u32[]{:S(2)}, u32[]{:S(2)}) collective-permute-start(bf16[256,2048]{1,0:T(8,128)(2,1)} %get-tuple-element.40), channel_id=1, source_target_pairs={{0,1},{1,0},{2,3},{3,2},{4,5},{5,4},{6,7},{7,6},{8,9},{9,8},{10,11... | collective-permute-start | bytes 3145736 | tf_op jit(solution)/shard_map/ppermute | solution.py:455
  (16 other events, 148.5 us)

commit v3 on v2

--- a/solution.py
+++ b/solution.py
@@ -15,8 +15,9 @@
 MASKED = -1e30
 LOG2E = 1.4426950408889634
 PLANE = 4
-ALONE = 52 * 1024 * 1024
+ALONE = 49 * 1024 * 1024
 GRANT = 24 * 1024 * 1024
+LAST = 42 * 1024 * 1024
 
 
 def turn(vectors, cosine, sine):
@@ -427,7 +428,7 @@
         out_shape=out_shape,
         input_output_aliases=aliases,
         compiler_params=pltpu.CompilerParams(
-            dimension_semantics=("arbitrary",), vmem_limit_bytes=ALONE if last else GRANT
+            dimension_semantics=("arbitrary",), vmem_limit_bytes=LAST if last else GRANT
         ),
         cost_estimate=pl.CostEstimate(
             flops=8 * columns * tokens * size * count,
@@ -450,6 +451,7 @@
     piece = tokens // parts
     cp_rank = lax.axis_index("cp")
     tp_rank = lax.axis_index("tp")
+    tp_info = jnp.full((1,), tp_rank, jnp.int32)
 
     def tp_shift(array, shift):
         return lax.ppermute(array, "tp", [(i, (i + shift) % n_tp) for i in range(n_tp)])
@@ -467,8 +469,9 @@
     running = counts
     reach = 1
     while reach < n_cp:
-        running = running + cp_shift(running, reach)
-        reach *= 2
+        further = [cp_shift(running, reach * times) for times in (1, 2, 3) if reach * times < n_cp]
+        running = sum(further, running)
+        reach *= 4
     before = running - counts
     base = cp_rank * tokens
     earlier = jnp.sum((doc_ids[None, :] < doc_ids[:, None]).astype(jnp.int32), axis=1)
@@ -512,7 +515,7 @@
             near[back].append(here)
             far[back].append(lax.ppermute(here, "cp", cross if back else own_cross))
         normed_parts.append(normed)
-    q_parts = product(normed_parts, w_query, info[15:], w_query.shape[1], (cosine, sine))
+    q_parts = product(normed_parts, w_query, jnp.zeros((1,), jnp.int32), w_query.shape[1], (cosine, sine))
     sets = []
     swap = [(i, i ^ 1) for i in range(n_cp)]
     for back in range(layers):
@@ -531,7 +534,7 @@
     for part in range(parts):
         attended, *partials = states[part]
         received = [tp_shift(partial, shift + 1) for shift, partial in enumerate(partials)]
-        own = product([attended], w_out, info[10:11] * features, features)[0]
+        own = product([attended], w_out, tp_info * features, features)[0]
         mixed = own.astype(jnp.float32)
         for other in received:
             mixed = mixed + other.astype(jnp.float32)

time: 297 us -> 294 us (0.990)
  starting transfers between devices: 33.1 us -> 40.7 us
  Pallas kernels: 156 us -> 150 us
  local copies, waits for them, and re-layouts: 12 us -> 6.7 us
    ppermute x4, starting transfers between devices: 6.81 us -> 14.1 us  [sublayer(): sets.append([local, lax.ppermute(local, 'cp', swap)])]
    pallas_call x3, Pallas kernels: 29.9 us -> 24.9 us  [product(): pl.pallas_call(functools.partial(product_kernel, block, len(xs), bool(tur...]
    unnamed x28 -> x26, local copies, waits for them, and re-layouts: 8.39 us -> 3.7 us
    ppermute x4, waiting for transfers between devices: 16.6 us -> 20.4 us  [tp_shift(): lax.ppermute(array, 'tp', [(i, (i + shift) % n_tp) for i in range(n_tp)])]
    ppermute x8, waiting for transfers between devices: 28.7 us -> 25.1 us  [sublayer(): far[back].append(lax.ppermute(here, 'cp', cross if back else own_cross))]
    ppermute x10 -> x12, starting transfers between devices: 13.2 us -> 15.7 us  [cp_shift(): lax.ppermute(array, 'cp', [(i, i + shift) for i in range(n_cp - shift)])]
    ppermute x10 -> x12, waiting for transfers between devices: 35.6 us -> 35.8 us  [cp_shift(): lax.ppermute(array, 'cp', [(i, i + shift) for i in range(n_cp - shift)])]
  transfers between devices with their start and end apart: 26 -> 28, of which waited for: 11 -> 13; matrix products, arithmetic and copies ran while one was open for 5% -> 5% of each run, Pallas kernels for 45% -> 44%
where the time goes in v3:
time: 294 us; the launch traced here: 293 us
  Pallas kernels  150 us (51%)
  waiting for transfers between devices  81.3 us (28%)
  starting transfers between devices  40.7 us (14%)
  other arithmetic  14.6 us (5%)
  local copies, waits for them, and re-layouts  6.7 us (2%)
    pallas_call x6, Pallas kernels, attend(): pl.pallas_call(functools.partial(attend_kernel, group, backs, part, first...  107 us
    ppermute x12, waiting for transfers between devices, cp_shift(): lax.ppermute(array, 'cp', [(i, i + shift) for i in range(n_cp - shift)])  35.8 us
    ppermute x8, waiting for transfers between devices, sublayer(): far[back].append(lax.ppermute(here, 'cp', cross if back else own_cross))  25.1 us
    pallas_call x3, Pallas kernels, product(): pl.pallas_call(functools.partial(product_kernel, block, len(xs), bool(tur...  24.9 us
    ppermute x4, waiting for transfers between devices, tp_shift(): lax.ppermute(array, 'tp', [(i, (i + shift) % n_tp) for i in range(n_tp)])  20.4 us
    pallas_call x2, Pallas kernels, project_keys(): pl.pallas_call(functools.partial(key_value_kernel, n_tp, block), in_specs...  17.9 us
    ppermute x12, starting transfers between devices, cp_shift(): lax.ppermute(array, 'cp', [(i, i + shift) for i in range(n_cp - shift)])  15.7 us
    ppermute x4, starting transfers between devices, sublayer(): sets.append([local, lax.ppermute(local, 'cp', swap)])  14.1 us
  transfers between devices with their start and end apart: 28, of which 13 were waited for; matrix products, arithmetic and copies ran while one was open for 5% of the time, Pallas kernels for 44%

profile of v3, /device:TPU:27, one launch (start us, length us, event | category | flops | bytes accessed | tf_op | source)
XLA Modules:
  0.0 293.3 jit_solution(7414748131418340243)
XLA Ops:
  14.2 3.2 %collective-permute-done.3 = s32[128]{0:T(128)S(1)} collective-permute-done((s32[128]{0:T(128)S(1)}, s32[128]{0:T(128)S(1)}, u32[]{:S(2)}, u32[]{:S(2)}) %collective-permute-start.3) | collective-permute-done | bytes 544 | tf_op jit(solution)/shard_map/ppermute | solution.py:460
  19.4 2.8 collective-permute-done.5
  30.3 10.3 %project_keys.3 = (bf16[4,256,256]{2,1,0:T(8,128)(2,1)S(1)}, bf16[256,4096]{1,0:T(8,128)(2,1)S(1)}) custom-call(s32[16]{0:T(128)S(1)} %compare_select_fusion.13.info, bf16[256,2048]{1,0:T(8,128)(2,1)S(1)} %get-tuple-element.41.refs_0_, bf16[256,2048]{1,0:T(8,128)(2,1)} %collective-permute-done.7.refs_1_, f32[1,4096]{1,0:T(1,128)S(1)} %bitcast.25, ...), custom_call_target="tpu_custom_call" | custom-call | flops 2147483648 | bytes 8388608 | tf_op jit(solution)/shard_map/project_keys/pallas_call | solution.py:94
  41.9 10.7 %collective-permute-done.6.refs_1_ = bf16[256,2048]{1,0:T(8,128)(2,1)S(1)} collective-permute-done((bf16[256,2048]{1,0:T(8,128)(2,1)S(1)}, bf16[256,2048]{1,0:T(8,128)(2,1)S(1)}, u32[]{:S(2)}, u32[]{:S(2)}) %collective-permute-start.6) | collective-permute-done | bytes 1048608 | tf_op jit(solution)/shard_map/ppermute | solution.py:457
  52.6 7.6 %project_keys.2 = (bf16[4,256,256]{2,1,0:T(8,128)(2,1)S(1)}, bf16[256,4096]{1,0:T(8,128)(2,1)S(1)}) custom-call(s32[16]{0:T(128)S(1)} %compare_select_fusion.13.info, bf16[256,2048]{1,0:T(8,128)(2,1)S(1)} %get-tuple-element.42.refs_0_, bf16[256,2048]{1,0:T(8,128)(2,1)S(1)} %collective-permute-done.6.refs_1_, f32[1,4096]{1,0:T(1,128)S(1)} %bitcast.26, ...), custom_call_target="tpu_custom_call" | custom-call | flops 2147483648 | bytes 8388608 | tf_op jit(solution)/shard_map/project_keys/pallas_call | solution.py:94
  65.5 3.7 %collective-permute-start.21 = (bf16[4,256,256]{2,1,0:T(8,128)(2,1)S(1)}, bf16[4,256,256]{2,1,0:T(8,128)(2,1)S(1)}, u32[]{:S(2)}, u32[]{:S(2)}) collective-permute-start(bf16[4,256,256]{2,1,0:T(8,128)(2,1)S(1)} %collective-permute-done.10), channel_id=1, source_target_pairs={{0,4},{2,6},{4,0},{6,2},{8,12},{10,14},{12,8},{14,10},{16,20},{18,... | collective-permute-start | bytes 1572872 | tf_op jit(solution)/shard_map/ppermute | solution.py:516
  70.4 10.1 %collective-permute-done.8 = bf16[4,256,256]{2,1,0:T(8,128)(2,1)S(1)} collective-permute-done((bf16[4,256,256]{2,1,0:T(8,128)(2,1)S(1)}, bf16[4,256,256]{2,1,0:T(8,128)(2,1)S(1)}, u32[]{:S(2)}, u32[]{:S(2)}) %collective-permute-start.8) | collective-permute-done | bytes 524320 | tf_op jit(solution)/shard_map/ppermute | solution.py:460
  82.0 7.4 %collective-permute-done.23 = bf16[4,256,256]{2,1,0:T(8,128)(2,1)S(1)} collective-permute-done((bf16[4,256,256]{2,1,0:T(8,128)(2,1)S(1)}, bf16[4,256,256]{2,1,0:T(8,128)(2,1)S(1)}, u32[]{:S(2)}, u32[]{:S(2)}) %collective-permute-start.23) | collective-permute-done | bytes 524320 | tf_op jit(solution)/shard_map/ppermute | solution.py:516
  89.6 4.6 %collective-permute-start.25 = (bf16[4,4,256,256]{3,2,1,0:T(8,128)(2,1)S(1)}, bf16[4,4,256,256]{3,2,1,0:T(8,128)(2,1)S(1)}, u32[]{:S(2)}, u32[]{:S(2)}) collective-permute-start(bf16[4,4,256,256]{3,2,1,0:T(8,128)(2,1)S(1)} %pad_maximum_fusion.3.refs_0_), channel_id=1, source_target_pairs={{0,2},{2,0},{4,6},{6,4},{8,10},{10,8},{12,14},{14,12},{16,18},{18,... | collective-permute-start | bytes 6291464 | tf_op jit(solution)/shard_map/ppermute | solution.py:523
  95.5 7.5 %collective-permute-done.9 = bf16[4,256,256]{2,1,0:T(8,128)(2,1)S(1)} collective-permute-done((bf16[4,256,256]{2,1,0:T(8,128)(2,1)S(1)}, bf16[4,256,256]{2,1,0:T(8,128)(2,1)S(1)}, u32[]{:S(2)}, u32[]{:S(2)}) %collective-permute-start.9) | collective-permute-done | bytes 524320 | tf_op jit(solution)/shard_map/ppermute | solution.py:460
  104.3 7.5 %collective-permute-done.20 = bf16[4,256,256]{2,1,0:T(8,128)(2,1)S(1)} collective-permute-done((bf16[4,256,256]{2,1,0:T(8,128)(2,1)S(1)}, bf16[4,256,256]{2,1,0:T(8,128)(2,1)S(1)}, u32[]{:S(2)}, u32[]{:S(2)}) %collective-permute-start.20) | collective-permute-done | bytes 524320 | tf_op jit(solution)/shard_map/ppermute | solution.py:516
  112.1 4.6 %collective-permute-start.22 = (bf16[4,4,256,256]{3,2,1,0:T(8,128)(2,1)S(1)}, bf16[4,4,256,256]{3,2,1,0:T(8,128)(2,1)}, u32[]{:S(2)}, u32[]{:S(2)}) collective-permute-start(bf16[4,4,256,256]{3,2,1,0:T(8,128)(2,1)S(1)} %pad_maximum_fusion.2.refs_0_), channel_id=1, source_target_pairs={{0,2},{2,0},{4,6},{6,4},{8,10},{10,8},{12,14},{14,12},{16,18},{18,... | collective-permute-start | bytes 6291464 | tf_op jit(solution)/shard_map/ppermute | solution.py:523
  116.7 8.9 %collective-permute-done.15 = bf16[4,256,256]{2,1,0:T(8,128)(2,1)} collective-permute-done((bf16[4,256,256]{2,1,0:T(8,128)(2,1)S(1)}, bf16[4,256,256]{2,1,0:T(8,128)(2,1)}, u32[]{:S(2)}, u32[]{:S(2)}) %collective-permute-start.15) | collective-permute-done | bytes 524320 | tf_op jit(solution)/shard_map/ppermute | solution.py:460
  127.0 15.8 %project_queries.1 = (bf16[256,2048]{1,0:T(8,128)(2,1)S(1)}, bf16[256,2048]{1,0:T(8,128)(2,1)S(1)}) custom-call(s32[1]{0:T(128)} %constant.51.clone.1.offset, f32[512,128]{1,0:T(8,128)S(1)} %get-tuple-element.48.refs_0_, f32[512,128]{1,0:T(8,128)S(1)} %get-tuple-element.47.refs_1_, bf16[256,4096]{1,0:T(8,128)(2,1)S(1)} %copy-done.3, ...), custom_call_target="tpu_custom_call" | custom-call | flops 8589934592 | bytes 16777216 | tf_op jit(solution)/shard_map/project_queries/pallas_call | solution.py:167
  146.5 10.3 %collective-permute-done.17 = bf16[4,256,256]{2,1,0:T(8,128)(2,1)S(1)} collective-permute-done((bf16[4,256,256]{2,1,0:T(8,128)(2,1)}, bf16[4,256,256]{2,1,0:T(8,128)(2,1)S(1)}, u32[]{:S(2)}, u32[]{:S(2)}) %collective-permute-start.17) | collective-permute-done | bytes 524320 | tf_op jit(solution)/shard_map/ppermute | solution.py:516
  160.7 16.3 %attend.6 = (f32[4,2,128,512]{3,2,1,0:T(8,128)S(1)}, f32[4,4,512]{2,1,0:T(4,128)S(1)}) custom-call(s32[16]{0:T(128)S(1)} %compare_select_fusion.13.info, s32[8,512]{1,0:T(8,128)S(1)} %broadcast_in_dim.80.start_ref, bf16[256,2048]{1,0:T(8,128)(2,1)S(1)} %copy-done.7, bf16[4,4,256,256]{3,2,1,0:T(8,128)(2,1)S(1)} %pad_maximum_fusion.3.refs_0_, ...), custom_call_target="tpu_custom_call" | custom-call | flops 8589934592 | bytes 8388608 | tf_op jit(solution)/shard_map/attend/pallas_call | solution.py:419
  177.0 16.4 %attend.9 = (f32[4,2,128,512]{3,2,1,0:T(8,128)S(1)}, f32[4,4,512]{2,1,0:T(4,128)S(1)}) custom-call(s32[16]{0:T(128)S(1)} %compare_select_fusion.13.info, s32[8,512]{1,0:T(8,128)S(1)} %broadcast_in_dim.80.start_ref, bf16[256,2048]{1,0:T(8,128)(2,1)S(1)} %copy-done.5, bf16[4,4,256,256]{3,2,1,0:T(8,128)(2,1)S(1)} %pad_maximum_fusion.3.refs_0_, ...), custom_call_target="tpu_custom_call" | custom-call | flops 8589934592 | bytes 8388608 | tf_op jit(solution)/shard_map/attend/pallas_call | solution.py:419
  193.4 15.8 %attend.7 = (f32[4,2,128,512]{3,2,1,0:T(8,128)S(1)}, f32[4,4,512]{2,1,0:T(4,128)S(1)}) custom-call(s32[16]{0:T(128)S(1)} %compare_select_fusion.13.info, s32[8,512]{1,0:T(8,128)S(1)} %broadcast_in_dim.80.start_ref, bf16[256,2048]{1,0:T(8,128)(2,1)S(1)} %copy-done.7, ...), custom_call_target="tpu_custom_call", output_to_operand_aliasing={{0}: (5, {}), {1}: (6, {})} | custom-call | flops 8589934592 | bytes 8388608 | tf_op jit(solution)/shard_map/attend/pallas_call | solution.py:419
  210.5 15.8 %attend.10 = (f32[4,2,128,512]{3,2,1,0:T(8,128)S(1)}, f32[4,4,512]{2,1,0:T(4,128)S(1)}) custom-call(s32[16]{0:T(128)S(1)} %compare_select_fusion.13.info, s32[8,512]{1,0:T(8,128)S(1)} %broadcast_in_dim.80.start_ref, bf16[256,2048]{1,0:T(8,128)(2,1)S(1)} %copy-done.5, ...), custom_call_target="tpu_custom_call", output_to_operand_aliasing={{0}: (5, {}), {1}: (6, {})} | custom-call | flops 8589934592 | bytes 8388608 | tf_op jit(solution)/shard_map/attend/pallas_call | solution.py:419
  226.3 21.3 %attend.8 = (bf16[256,2048]{1,0:T(8,128)(2,1)S(1)}, bf16[256,2048]{1,0:T(8,128)(2,1)}) custom-call(s32[16]{0:T(128)S(1)} %compare_select_fusion.13.info, s32[8,512]{1,0:T(8,128)S(1)} %broadcast_in_dim.80.start_ref, bf16[256,2048]{1,0:T(8,128)(2,1)S(1)} %copy-done.7, bf16[4,4,256,256]{3,2,1,0:T(8,128)(2,1)S(1)} %pad_maximum_fusion.refs_0_, ...), custom_call_target="tpu_custom_call" | custom-call | flops 17179869184 | bytes 8388608 | tf_op jit(solution)/shard_map/attend/pallas_call | solution.py:419
  249.0 21.1 %attend.11 = (bf16[256,2048]{1,0:T(8,128)(2,1)S(1)}, bf16[256,2048]{1,0:T(8,128)(2,1)}) custom-call(s32[16]{0:T(128)S(1)} %compare_select_fusion.13.info, s32[8,512]{1,0:T(8,128)S(1)} %broadcast_in_dim.80.start_ref, bf16[256,2048]{1,0:T(8,128)(2,1)S(1)} %copy-done.5, bf16[4,4,256,256]{3,2,1,0:T(8,128)(2,1)S(1)} %pad_maximum_fusion.refs_0_, ...), custom_call_target="tpu_custom_call" | custom-call | flops 17179869184 | bytes 8388608 | tf_op jit(solution)/shard_map/attend/pallas_call | solution.py:419
  270.4 4.6 %partial_product.2 = bf16[256,2048]{1,0:T(8,128)(2,1)S(1)} custom-call(s32[1]{0:T(128)} %bitcast.offset, bf16[256,2048]{1,0:T(8,128)(2,1)S(1)} %get-tuple-element.32.refs_0_, bf16[2048,4096]{1,0:T(8,128)(2,1)} %refs_1_.3), custom_call_target="tpu_custom_call" | custom-call | flops 2147483648 | bytes 8388608 | tf_op jit(solution)/shard_map/partial_product/pallas_call | solution.py:167
  275.0 4.6 %partial_product.3 = bf16[256,2048]{1,0:T(8,128)(2,1)S(1)} custom-call(s32[1]{0:T(128)} %bitcast.offset, bf16[256,2048]{1,0:T(8,128)(2,1)S(1)} %get-tuple-element.39.refs_0_, bf16[2048,4096]{1,0:T(8,128)(2,1)} %refs_1_.3), custom_call_target="tpu_custom_call" | custom-call | flops 2147483648 | bytes 8388608 | tf_op jit(solution)/shard_map/partial_product/pallas_call | solution.py:167
  281.3 8.8 %collective-permute-done.27 = bf16[256,2048]{1,0:T(8,128)(2,1)} collective-permute-done((bf16[256,2048]{1,0:T(8,128)(2,1)}, bf16[256,2048]{1,0:T(8,128)(2,1)}, u32[]{:S(2)}, u32[]{:S(2)}) %collective-permute-start.27) | collective-permute-done | bytes 1048608 | tf_op jit(solution)/shard_map/ppermute | solution.py:457
  (90 shorter events, 53.5 us)
Async XLA Ops:
  0.9 8.1 %collective-permute-start = (s32[128]{0:T(128)S(1)}, s32[128]{0:T(128)S(1)}, u32[]{:S(2)}, u32[]{:S(2)}) collective-permute-start(s32[128]{0:T(128)S(1)} %convert_reduce_fusion.1), channel_id=1, source_target_pairs={{0,2},{2,4},{4,6},{6,8},{8,10},{10,12},{12,14},{14,16},{16,18},{18... | collective-permute-start | bytes 1544 | tf_op jit(solution)/shard_map/ppermute | solution.py:460
  6.7 23.6 %collective-permute-start.7 = (bf16[256,2048]{1,0:T(8,128)(2,1)S(1)}, bf16[256,2048]{1,0:T(8,128)(2,1)}, u32[]{:S(2)}, u32[]{:S(2)}) collective-permute-start(bf16[256,2048]{1,0:T(8,128)(2,1)S(1)} %get-tuple-element.41.refs_0_), channel_id=1, source_target_pairs={{0,1},{1,0},{2,3},{3,2},{4,5},{5,4},{6,7},{7,6},{8,9},{9,8},{10,11... | collective-permute-start | bytes 3145736 | tf_op jit(solution)/shard_map/ppermute | solution.py:457
  8.0 44.6 %collective-permute-start.6 = (bf16[256,2048]{1,0:T(8,128)(2,1)S(1)}, bf16[256,2048]{1,0:T(8,128)(2,1)S(1)}, u32[]{:S(2)}, u32[]{:S(2)}) collective-permute-start(bf16[256,2048]{1,0:T(8,128)(2,1)S(1)} %get-tuple-element.42.refs_0_), channel_id=1, source_target_pairs={{0,1},{1,0},{2,3},{3,2},{4,5},{5,4},{6,7},{7,6},{8,9},{9,8},{10,11... | collective-permute-start | bytes 3145736 | tf_op jit(solution)/shard_map/ppermute | solution.py:457
  12.9 9.4 %collective-permute-start.5 = (s32[128]{0:T(128)S(1)}, s32[128]{0:T(128)S(1)}, u32[]{:S(2)}, u32[]{:S(2)}) collective-permute-start(s32[128]{0:T(128)S(1)} %add_add_fusion), channel_id=1, source_target_pairs={{0,24},{2,26},{4,28},{6,30},{1,25},{3,27},{5,29},{7,31}} | collective-permute-start | bytes 1544 | tf_op jit(solution)/shard_map/ppermute | solution.py:460
  40.6 24.8 %collective-permute-start.10 = (bf16[4,256,256]{2,1,0:T(8,128)(2,1)S(1)}, bf16[4,256,256]{2,1,0:T(8,128)(2,1)S(1)}, u32[]{:S(2)}, u32[]{:S(2)}) collective-permute-start(bf16[4,256,256]{2,1,0:T(8,128)(2,1)S(1)} %get-tuple-element.27), channel_id=1, source_target_pairs={{0,8},{2,10},{4,12},{6,14},{8,16},{10,18},{12,20},{14,22},{16,24},... | collective-permute-start | bytes 1572872 | tf_op jit(solution)/shard_map/ppermute | solution.py:460
  61.6 18.9 %collective-permute-start.8 = (bf16[4,256,256]{2,1,0:T(8,128)(2,1)S(1)}, bf16[4,256,256]{2,1,0:T(8,128)(2,1)S(1)}, u32[]{:S(2)}, u32[]{:S(2)}) collective-permute-start(bf16[4,256,256]{2,1,0:T(8,128)(2,1)S(1)} %get-tuple-element.26), channel_id=1, source_target_pairs={{0,8},{2,10},{4,12},{6,14},{8,16},{10,18},{12,20},{14,22},{16,24},... | collective-permute-start | bytes 1572872 | tf_op jit(solution)/shard_map/ppermute | solution.py:460
  62.8 19.1 %collective-permute-start.24 = (bf16[4,256,256]{2,1,0:T(8,128)(2,1)S(1)}, bf16[4,256,256]{2,1,0:T(8,128)(2,1)S(1)}, u32[]{:S(2)}, u32[]{:S(2)}) collective-permute-start(bf16[4,256,256]{2,1,0:T(8,128)(2,1)S(1)} %get-tuple-element.27), channel_id=1, source_target_pairs={{0,4},{2,6},{8,12},{10,14},{16,20},{18,22},{24,28},{26,30},{1,5},{... | collective-permute-start | bytes 1572872 | tf_op jit(solution)/shard_map/ppermute | solution.py:516
  64.1 25.2 %collective-permute-start.23 = (bf16[4,256,256]{2,1,0:T(8,128)(2,1)S(1)}, bf16[4,256,256]{2,1,0:T(8,128)(2,1)S(1)}, u32[]{:S(2)}, u32[]{:S(2)}) collective-permute-start(bf16[4,256,256]{2,1,0:T(8,128)(2,1)S(1)} %get-tuple-element.26), channel_id=1, source_target_pairs={{0,4},{2,6},{8,12},{10,14},{16,20},{18,22},{24,28},{26,30},{1,5},{... | collective-permute-start | bytes 1572872 | tf_op jit(solution)/shard_map/ppermute | solution.py:516
  65.5 38.8 %collective-permute-start.21 = (bf16[4,256,256]{2,1,0:T(8,128)(2,1)S(1)}, bf16[4,256,256]{2,1,0:T(8,128)(2,1)S(1)}, u32[]{:S(2)}, u32[]{:S(2)}) collective-permute-start(bf16[4,256,256]{2,1,0:T(8,128)(2,1)S(1)} %collective-permute-done.10), channel_id=1, source_target_pairs={{0,4},{2,6},{4,0},{6,2},{8,12},{10,14},{12,8},{14,10},{16,20},{18,... | collective-permute-start | bytes 1572872 | tf_op jit(solution)/shard_map/ppermute | solution.py:516
  69.1 25.0 %collective-permute-start.11 = (bf16[4,256,256]{2,1,0:T(8,128)(2,1)S(1)}, bf16[4,256,256]{2,1,0:T(8,128)(2,1)S(1)}, u32[]{:S(2)}, u32[]{:S(2)}) collective-permute-start(bf16[4,256,256]{2,1,0:T(8,128)(2,1)S(1)} %collective-permute-done.10), channel_id=1, source_target_pairs={{0,8},{2,10},{4,12},{6,14},{8,16},{10,18},{12,20},{14,22},{16,24},... | collective-permute-start | bytes 1572872 | tf_op jit(solution)/shard_map/ppermute | solution.py:460
  80.5 22.5 %collective-permute-start.9 = (bf16[4,256,256]{2,1,0:T(8,128)(2,1)S(1)}, bf16[4,256,256]{2,1,0:T(8,128)(2,1)S(1)}, u32[]{:S(2)}, u32[]{:S(2)}) collective-permute-start(bf16[4,256,256]{2,1,0:T(8,128)(2,1)S(1)} %collective-permute-done.8), channel_id=1, source_target_pairs={{0,8},{2,10},{4,12},{6,14},{8,16},{10,18},{12,20},{14,22},{16,24},... | collective-permute-start | bytes 1572872 | tf_op jit(solution)/shard_map/ppermute | solution.py:460
  89.6 71.1 %collective-permute-start.25 = (bf16[4,4,256,256]{3,2,1,0:T(8,128)(2,1)S(1)}, bf16[4,4,256,256]{3,2,1,0:T(8,128)(2,1)S(1)}, u32[]{:S(2)}, u32[]{:S(2)}) collective-permute-start(bf16[4,4,256,256]{3,2,1,0:T(8,128)(2,1)S(1)} %pad_maximum_fusion.3.refs_0_), channel_id=1, source_target_pairs={{0,2},{2,0},{4,6},{6,4},{8,10},{10,8},{12,14},{14,12},{16,18},{18,... | collective-permute-start | bytes 6291464 | tf_op jit(solution)/shard_map/ppermute | solution.py:523
  94.2 17.6 %collective-permute-start.20 = (bf16[4,256,256]{2,1,0:T(8,128)(2,1)S(1)}, bf16[4,256,256]{2,1,0:T(8,128)(2,1)S(1)}, u32[]{:S(2)}, u32[]{:S(2)}) collective-permute-start(bf16[4,256,256]{2,1,0:T(8,128)(2,1)S(1)} %collective-permute-done.8), channel_id=1, source_target_pairs={{0,4},{2,6},{4,0},{6,2},{8,12},{10,14},{12,8},{14,10},{16,20},{18,... | collective-permute-start | bytes 1572872 | tf_op jit(solution)/shard_map/ppermute | solution.py:516
  94.2 22.5 %collective-permute-start.16 = (bf16[4,256,256]{2,1,0:T(8,128)(2,1)S(1)}, bf16[4,256,256]{2,1,0:T(8,128)(2,1)S(1)}, u32[]{:S(2)}, u32[]{:S(2)}) collective-permute-start(bf16[4,256,256]{2,1,0:T(8,128)(2,1)S(1)} %collective-permute-done.11), channel_id=1, source_target_pairs={{0,8},{2,10},{4,12},{6,14},{8,16},{10,18},{12,20},{14,22},{16,24},... | collective-permute-start | bytes 1572872 | tf_op jit(solution)/shard_map/ppermute | solution.py:460
  102.9 22.6 %collective-permute-start.15 = (bf16[4,256,256]{2,1,0:T(8,128)(2,1)S(1)}, bf16[4,256,256]{2,1,0:T(8,128)(2,1)}, u32[]{:S(2)}, u32[]{:S(2)}) collective-permute-start(bf16[4,256,256]{2,1,0:T(8,128)(2,1)S(1)} %collective-permute-done.9), channel_id=1, source_target_pairs={{0,8},{2,10},{4,12},{6,14},{8,16},{10,18},{12,20},{14,22},{16,24},... | collective-permute-start | bytes 1572872 | tf_op jit(solution)/shard_map/ppermute | solution.py:460
  104.2 21.9 %collective-permute-start.13 = (bf16[4,256,256]{2,1,0:T(8,128)(2,1)S(1)}, bf16[4,256,256]{2,1,0:T(8,128)(2,1)S(1)}, u32[]{:S(2)}, u32[]{:S(2)}) collective-permute-start(bf16[4,256,256]{2,1,0:T(8,128)(2,1)S(1)} %collective-permute-done.11), channel_id=1, source_target_pairs={{0,4},{2,6},{4,0},{6,2},{8,12},{10,14},{12,8},{14,10},{16,20},{18,... | collective-permute-start | bytes 1572872 | tf_op jit(solution)/shard_map/ppermute | solution.py:516
  112.1 81.3 %collective-permute-start.22 = (bf16[4,4,256,256]{3,2,1,0:T(8,128)(2,1)S(1)}, bf16[4,4,256,256]{3,2,1,0:T(8,128)(2,1)}, u32[]{:S(2)}, u32[]{:S(2)}) collective-permute-start(bf16[4,4,256,256]{3,2,1,0:T(8,128)(2,1)S(1)} %pad_maximum_fusion.2.refs_0_), channel_id=1, source_target_pairs={{0,2},{2,0},{4,6},{6,4},{8,10},{10,8},{12,14},{14,12},{16,18},{18,... | collective-permute-start | bytes 6291464 | tf_op jit(solution)/shard_map/ppermute | solution.py:523
  116.6 26.1 %collective-permute-start.12 = (bf16[4,256,256]{2,1,0:T(8,128)(2,1)S(1)}, bf16[4,256,256]{2,1,0:T(8,128)(2,1)S(1)}, u32[]{:S(2)}, u32[]{:S(2)}) collective-permute-start(bf16[4,256,256]{2,1,0:T(8,128)(2,1)S(1)} %collective-permute-done.9), channel_id=1, source_target_pairs={{0,4},{2,6},{4,0},{6,2},{8,12},{10,14},{12,8},{14,10},{16,20},{18,... | collective-permute-start | bytes 1572872 | tf_op jit(solution)/shard_map/ppermute | solution.py:516
  125.5 21.0 %collective-permute-start.18 = (bf16[4,256,256]{2,1,0:T(8,128)(2,1)S(1)}, bf16[4,256,256]{2,1,0:T(8,128)(2,1)S(1)}, u32[]{:S(2)}, u32[]{:S(2)}) collective-permute-start(bf16[4,256,256]{2,1,0:T(8,128)(2,1)S(1)} %collective-permute-done.16), channel_id=1, source_target_pairs={{0,4},{2,6},{4,0},{6,2},{8,12},{10,14},{12,8},{14,10},{16,20},{18,... | collective-permute-start | bytes 1572872 | tf_op jit(solution)/shard_map/ppermute | solution.py:516
  126.1 30.6 %collective-permute-start.17 = (bf16[4,256,256]{2,1,0:T(8,128)(2,1)}, bf16[4,256,256]{2,1,0:T(8,128)(2,1)S(1)}, u32[]{:S(2)}, u32[]{:S(2)}) collective-permute-start(bf16[4,256,256]{2,1,0:T(8,128)(2,1)} %collective-permute-done.15), channel_id=1, source_target_pairs={{0,4},{2,6},{4,0},{6,2},{8,12},{10,14},{12,8},{14,10},{16,20},{18,... | collective-permute-start | bytes 1572872 | tf_op jit(solution)/shard_map/ppermute | solution.py:516
  144.1 82.2 %collective-permute-start.14 = (bf16[4,4,256,256]{3,2,1,0:T(8,128)(2,1)S(1)}, bf16[4,4,256,256]{3,2,1,0:T(8,128)(2,1)S(1)}, u32[]{:S(2)}, u32[]{:S(2)}) collective-permute-start(bf16[4,4,256,256]{3,2,1,0:T(8,128)(2,1)S(1)} %pad_maximum_fusion.refs_0_), channel_id=1, source_target_pairs={{0,2},{2,0},{4,6},{6,4},{8,10},{10,8},{12,14},{14,12},{16,18},{18,... | collective-permute-start | bytes 6291464 | tf_op jit(solution)/shard_map/ppermute | solution.py:523
  158.1 68.2 %collective-permute-start.19 = (bf16[4,4,256,256]{3,2,1,0:T(8,128)(2,1)S(1)}, bf16[4,4,256,256]{3,2,1,0:T(8,128)(2,1)S(1)}, u32[]{:S(2)}, u32[]{:S(2)}) collective-permute-start(bf16[4,4,256,256]{3,2,1,0:T(8,128)(2,1)S(1)} %pad_maximum_fusion.1.refs_2_), channel_id=1, source_target_pairs={{0,2},{2,0},{4,6},{6,4},{8,10},{10,8},{12,14},{14,12},{16,18},{18,... | collective-permute-start | bytes 6291464 | tf_op jit(solution)/shard_map/ppermute | solution.py:523
  247.7 31.9 %collective-permute-start.26 = (bf16[256,2048]{1,0:T(8,128)(2,1)}, bf16[256,2048]{1,0:T(8,128)(2,1)}, u32[]{:S(2)}, u32[]{:S(2)}) collective-permute-start(bf16[256,2048]{1,0:T(8,128)(2,1)} %get-tuple-element.33), channel_id=1, source_target_pairs={{0,1},{1,0},{2,3},{3,2},{4,5},{5,4},{6,7},{7,6},{8,9},{9,8},{10,11... | collective-permute-start | bytes 3145736 | tf_op jit(solution)/shard_map/ppermute | solution.py:457
  270.1 20.0 %collective-permute-start.27 = (bf16[256,2048]{1,0:T(8,128)(2,1)}, bf16[256,2048]{1,0:T(8,128)(2,1)}, u32[]{:S(2)}, u32[]{:S(2)}) collective-permute-start(bf16[256,2048]{1,0:T(8,128)(2,1)} %get-tuple-element.40), channel_id=1, source_target_pairs={{0,1},{1,0},{2,3},{3,2},{4,5},{5,4},{6,7},{7,6},{8,9},{9,8},{10,11... | collective-permute-start | bytes 3145736 | tf_op jit(solution)/shard_map/ppermute | solution.py:457
  (17 other events, 186.6 us)
